TPU v7x, 256 devices: a 8x8x2 block of a 8x8x16 slice. The times are simulated.
256 devices in a mesh: groups: 2 (over z), kv: 128 (over y, x, core).
Axes of the slice: x: 8, y: 8, z: 2, core: 2. Of those that a mesh axis runs over, the one named last changes fastest.
The devices are a block of a 8x8x16 slice.
Arguments:
- queries: bfloat16 [80, 18432], P('groups', 'kv'), parts along dimension 0, may hold values from -240 to 240
- latent_cache: bfloat16 [80, 16384, 576], P('groups', 'kv'), parts along dimension 0, may hold values from -6 to 6
- context_lengths: int32 [80], P('groups'), parts along dimension 0, may hold values from 128 to 16384, as said below
- value_up: bfloat16 [16384, 128], P('kv'), may hold values from -0.25 to 0.25
- out_proj: bfloat16 [4096, 7168], P('kv'), may hold values from -0.09375 to 0.09375
- residual: bfloat16 [80, 7168], P('groups', 'kv'), parts along dimension 0, may hold values from -0.75 to 0.75
- norm_gain: bfloat16 [7168], P('kv'), may hold values from 0.5 to 1.5
- expert_ids: int32 [80, 8], P('groups'), parts along dimension 0, may hold values from 0 to 255, all different within a row; in each aligned block of 40 rows (0 to 39, 40 to 79, ...) at most 2 rows name the same one
- gate_weights: float32 [80, 8], P('groups'), parts along dimension 0, may hold values from 0.05 to 0.5
Outputs:
- dispatched: bfloat16 [512, 2, 7168], P(('groups', 'kv')), parts along dimension 0
- slot_scale: float32 [512, 2], P(('groups', 'kv')), parts along dimension 0
- slot_gate: float32 [512, 2], P(('groups', 'kv')), parts along dimension 0
There are 2 independent parts, one for each index of `groups`. A program takes and returns all parts, laid end to end along the dimension named above; an argument that names none is the same for every part. Nothing has to cross between parts.
Inputs may be any that keep to these rules, and one draw needn't show every extreme that they name: `context_lengths`: multiples of 128; some sequence is 16384 long. `expert_ids`: each token names 8 different experts; no expert is named by more than 2 tokens, a bound that some block reaches.
All inputs are finite; a program needn't handle non-finite values. Where the computation divides by a largest or mean magnitude, that divisor is 1e-20 or more.
Results may differ from a plain program's by a relative error of at most 0.0069.
Values may be sent and summed in bfloat16 or wider, within the bound.
A program may use at most 64 MiB of HBM per device.

v0:
```python
import jax
import jax.numpy as jnp
from jax import lax
from jax.sharding import Mesh
from jax.sharding import PartitionSpec as P

H = 32
LAT = 512
ROPE = 64
VD = 128
D = 7168
EXPERTS = 256
TOPK = 8
CAP = 2
KV = ("kv_0", "kv_1", "kv_2")
GROUPS_KV = ("groups", "kv_0", "kv_1", "kv_2")


score_scale = 192.0 ** (-0.5)
masked_score = -1e30
small_eps = 1e-06


def side_by_side(arrays, axis, dim, along):
    widths = [a.shape[along] for a in arrays]
    both = jnp.concatenate(arrays, axis=along)
    result = lax.all_gather(both, axis, axis=dim, tiled=True)
    return tuple(jnp.split(result, [sum(widths[:k]) for k in range(1, len(widths))], axis=along))


def in_blocks(value, dim, size):
    lengths = value.shape
    blocks = value.reshape(*lengths[:dim], size, lengths[dim] // size, *lengths[dim + 1 :])
    return jnp.moveaxis(blocks, dim, 0)


def in_order(blocks, dim):
    lengths = list(blocks.shape[1:])
    lengths[dim] *= blocks.shape[0]
    return jnp.moveaxis(blocks, 0, dim).reshape(lengths)


def moved_by_axis(blocks, axes, order):
    inside = blocks.shape[1:]
    result = blocks.reshape(*(lax.axis_size(a) for a in axes), *inside)
    for k in order:
        result = lax.all_to_all(result, axes[k], k, k, tiled=True)
    return result.reshape(-1, *inside)


def exchange_by_chip(value, groups, order, split_dim, concat_dim):
    size = lax.axis_size(groups[0]) * lax.axis_size(groups[1])
    blocks = in_blocks(value, split_dim, size)
    return in_order(moved_by_axis(blocks, groups, order), concat_dim)


def from_partner(value, axis, bit):
    mask = 2**bit
    pairs = [(source, source ^ mask) for source in range(lax.axis_size(axis))]
    return lax.ppermute(value, axis, pairs)


def gather_turned(arrays, axis, dims):
    turned = [jnp.moveaxis(a, dim, 0) for a, dim in zip(arrays, dims)]
    widths = [t[0].size for t in turned]
    both = jnp.concatenate([t.reshape(-1, w) for t, w in zip(turned, widths)], axis=1)
    result = lax.all_gather(both, axis, axis=0, tiled=True)
    blocks = jnp.split(result, [sum(widths[:k]) for k in range(1, len(widths))], axis=1)
    return tuple(
        (
            jnp.moveaxis(b.reshape(-1, *t.shape[1:]), 0, dim)
            for b, t, dim in zip(blocks, turned, dims)
        )
    )


def slot_targets(expert_ids):
    flat_ids = expert_ids.reshape(-1)
    order_index = jnp.arange(flat_ids.shape[0], dtype=jnp.int32)
    same_before = (flat_ids[:, None] == flat_ids[None, :]) & (
        order_index[None, :] < order_index[:, None]
    )
    rank_within = jnp.sum(same_before.astype(jnp.int32), axis=1)
    return flat_ids * CAP + rank_within


def slot_match(targets, first_slot, slot_count):
    slot_index = first_slot + jnp.arange(slot_count, dtype=jnp.int32)
    return (slot_index[:, None] == targets[None, :]).astype(jnp.float32)


def token_picker(matches, seq_count):
    return jnp.sum(matches.reshape(matches.shape[0], seq_count, TOPK), axis=2)


def per_device(
    queries,
    latent_cache,
    context_lengths,
    value_up,
    out_proj,
    residual,
    norm_gain,
    expert_ids,
    gate_weights,
):
    kv_count = lax.axis_size(KV)
    shard_index = lax.axis_index(KV)
    seq_count = queries.shape[0]
    query_rows = lax.all_gather(queries, KV, axis=1, tiled=True).reshape(seq_count, H, LAT + ROPE)
    ctx_local = latent_cache.shape[1]
    scores = (
        jnp.einsum("shq,scq->shc", query_rows, latent_cache, preferred_element_type=jnp.float32)
        * score_scale
    )
    position = shard_index * ctx_local + jnp.arange(ctx_local, dtype=jnp.int32)
    valid_mask = (position[None, :] < context_lengths[:, None])[:, None, :]
    scores = jnp.where(valid_mask, scores, masked_score)
    local_max = jnp.max(scores, axis=2)
    weights = jnp.where(valid_mask, jnp.exp(scores - local_max[:, :, None]), 0.0)
    local_total = jnp.sum(weights, axis=2)
    local_out = jnp.einsum(
        "shc,scl->shl",
        weights.astype(jnp.bfloat16),
        latent_cache[:, :, :LAT],
        preferred_element_type=jnp.float32,
    )
    out_rows = out_proj.shape[0]
    col_count = H * LAT // kv_count
    segment = min(col_count, LAT)
    head_count = col_count // segment
    head_start = shard_index * col_count // LAT
    every_max, every_total = side_by_side((local_max[None], local_total[None]), KV, 0, 1)
    global_max = jnp.max(every_max, axis=0)
    scaling = jnp.exp(every_max - global_max[None])
    weight_total = jnp.sum(every_total * scaling, axis=0)
    pieces = exchange_by_chip(
        local_out.reshape(1, seq_count, H * LAT).astype(jnp.bfloat16),
        (("kv_0", "kv_1"), "kv_2"),
        (1, 0),
        2,
        0,
    ).astype(jnp.float32)
    pieces = pieces.reshape(kv_count, seq_count, head_count, segment)
    own_scaling = lax.dynamic_slice_in_dim(scaling, head_start, head_count, 2)
    merged_sum = jnp.sum(pieces * own_scaling[:, :, :, None], axis=0)
    own_total = lax.dynamic_slice_in_dim(weight_total, head_start, head_count, 1)
    merged = merged_sum / own_total[:, :, None]
    projector = value_up.reshape(head_count, segment, VD).astype(jnp.float32)
    value_part = jnp.einsum("shl,hlv->shv", merged, projector, precision=lax.Precision.HIGHEST)
    holders = kv_count // H
    for bit in range(holders.bit_length() - 1):
        value_part = value_part + from_partner(value_part, KV, bit)
    value_rows = value_part.astype(jnp.bfloat16).reshape(seq_count, head_count * VD)
    value_rows = lax.dynamic_slice_in_dim(value_rows, shard_index % holders * out_rows, out_rows, 1)
    partial_out = jnp.dot(value_rows, out_proj, preferred_element_type=jnp.float32)
    experts_local = EXPERTS // kv_count
    slot_count = experts_local * CAP
    targets = slot_targets(expert_ids)
    own_match = slot_match(targets, shard_index * slot_count, slot_count)
    own_pick = token_picker(own_match, seq_count)
    slot_gate = jnp.dot(own_match, gate_weights.reshape(-1), precision=lax.Precision.HIGHEST)
    attn_rows = lax.psum(partial_out, KV)
    resid_rows, gain_cols = gather_turned((residual, norm_gain), KV, (1, 0))
    summed = attn_rows + resid_rows.astype(jnp.float32)
    inverse_rms = lax.rsqrt(jnp.mean(summed * summed, axis=1) + small_eps)
    normed = summed * inverse_rms[:, None] * gain_cols.astype(jnp.float32)
    peak_abs = jnp.max(jnp.abs(normed), axis=1) + small_eps
    coded_rows = (normed / peak_abs[:, None]).astype(jnp.bfloat16)
    dispatched = jnp.dot(
        own_pick.astype(jnp.bfloat16), coded_rows, preferred_element_type=jnp.float32
    ).astype(jnp.bfloat16)
    slot_scale = jnp.dot(own_pick, peak_abs, precision=lax.Precision.HIGHEST)
    return (
        dispatched.reshape(experts_local, CAP, D),
        slot_scale.reshape(experts_local, CAP),
        slot_gate.reshape(experts_local, CAP),
    )


def solution(mesh):
    split = Mesh(
        mesh.devices.reshape(mesh.shape["groups"], 8, 8, 2), ("groups", "kv_0", "kv_1", "kv_2")
    )
    in_specs = (
        P("groups", KV),
        P("groups", KV, None),
        P("groups"),
        P(KV, None),
        P(KV, None),
        P("groups", KV),
        P(KV),
        P("groups", None),
        P("groups", None),
    )
    out_specs = (P(GROUPS_KV, None, None), P(GROUPS_KV, None), P(GROUPS_KV, None))
    return jax.shard_map(
        per_device, mesh=split, in_specs=in_specs, out_specs=out_specs, check_vma=False
    )
```

profile of v0, /device:TPU:513, one launch (start us, length us, event | category | flops | bytes accessed | tf_op | source)
XLA Modules:
  0.0 446.8 jit_solution(12397648085348938041)
XLA Ops:
  7.2 0.0 copy-start
  7.2 0.1 all-gather.7.cloned.1.call-start
  7.3 0.7 all-gather.7.cloned.1.call-update
  8.0 0.1 all-gather.5.cloned.1.call-start
  8.1 0.7 broadcast_compare_fusion
  8.8 101.1 %all-gather.7.cloned.1.call-done = bf16[128,144,40]{1,2,0:T(8,128)(2,1)} async-done(((bf16[1,144,40]{1,2,0:T(8,128)(2,1)}), bf16[128,144,40]{1,2,0:T(8,128)(2,1)}) %all-gather.7.cloned.1.call-update) | async-done | bytes 1474576 | tf_op jit(solution)/shard_map/all_gather | solution.py:110
  109.9 2.3 copy.70
  112.2 6.1 %reshape.174 = bf16[18432,40]{0,1:T(8,128)(2,1)} reshape(bf16[128,144,40]{1,0,2:T(8,128)(2,1)S(1)} %copy.70) | data formatting | bytes 2949120
  118.3 3.3 reshape.167
  121.6 0.0 copy-start.4
  121.6 3.8 fusion.30
  125.5 0.1 copy.75
  125.6 0.5 fusion.7
  126.0 0.1 copy.76
  126.1 0.7 pad_maximum_fusion
  126.8 0.1 all-gather.5.cloned.1.call-update
  126.8 0.0 copy-done.4
  126.8 0.1 copy.68
  126.9 0.1 eq.43
  127.0 4.4 fusion.3
  131.5 0.8 convert_element_type.64
  132.3 0.8 copy.72
  133.1 0.3 copy.73
  133.5 4.8 %all_to_all.10 = bf16[64,2,1,40,128]{4,0,3,2,1:T(8,128)(2,1)S(1)} all-to-all(bf16[64,2,1,40,128]{4,0,3,2,1:T(8,128)(2,1)S(1)} %copy.73), channel_id=1, replica_groups=mesh['groups'=2,'kv_0'=8,'kv_1'=8,'kv_2'=2] {'kv_2'}, dimensions={1} | all-to-all | bytes 2621440 | tf_op jit(solution)/shard_map/all_to_all | solution.py:47
  138.3 2.4 copy.74
  140.7 10.7 %all-to-all-start.1 = ((bf16[64,2,1,40,128]{4,1,3,2,0:T(2,128)(2,1)}), bf16[64,2,1,40,128]{4,1,3,2,0:T(2,128)(2,1)S(1)}, u32[]{:S(2)}, u32[]{:S(2)}) async-start(bf16[64,2,1,40,128]{4,1,3,2,0:T(2,128)(2,1)} %copy.74), calls=%async_computation.1 | async-start | bytes 2621440 | tf_op jit(solution)/shard_map/all_to_all | solution.py:47
  151.4 0.1 all-reduce.2.cloned.1.call-start
  151.5 0.2 convert_reduce_fusion
  151.7 0.1 reduce_sum.57
  151.8 0.1 copy.69
  151.9 0.0 copy-done.5
  151.9 0.0 copy-done.7
  151.9 75.2 %all-gather.1 = bf16[128,56,41]{1,2,0:T(8,128)(2,1)S(1)} all-gather(bf16[1,56,41]{1,2,0:T(8,128)(2,1)S(1)} %maximum_bitcast_fusion), channel_id=1, replica_groups=mesh['groups'=2,'kv_0'=8,'kv_1'=8,'kv_2'=2] {'kv_0','kv_1','kv_2'}, dimensions={0}, use_global_device_ids=true | all-gather | bytes 592368 | tf_op jit(solution)/shard_map/all_gather | solution.py:67
  227.1 0.4 copy.78
  227.5 3.2 reshape.176
  230.7 0.9 slice_convert_fusion
  231.6 0.0 all-gather.5.cloned.1.call-done
  231.7 1.9 slice_reduce_fusion
  233.6 0.3 copy-done.1
  233.9 0.7 fusion.2
  234.6 0.1 constant_dynamic-slice_fusion.1
  234.6 0.5 copy.77
  235.2 0.0 copy-start.8
  235.2 0.0 all-to-all-done.1
  235.2 3.3 multiply_reduce_fusion
  238.5 0.2 convolution_bitcast_fusion
  238.8 0.3 collective-permute-start
  239.1 1.0 collective-permute-done
  240.1 1.1 collective-permute-start.1
  241.2 1.5 collective-permute-done.1
  242.7 0.0 copy-done
  242.7 1.4 fusion.19
  244.1 0.1 all-reduce.2.cloned.1.call-update
  244.2 0.1 copy.79
  244.3 0.1 reshape.179
  244.4 0.1 convert_reduce_fusion.1
  244.5 0.9 fusion.16
  245.3 191.1 %all-reduce.2.cloned.1.call-done = f32[40,7168]{1,0:T(8,128)} async-done(((f32[40,7168]{1,0:T(8,128)}), f32[40,7168]{1,0:T(8,128)}) %all-reduce.2.cloned.1.call-update) | async-done | bytes 1146896 | tf_op jit(solution)/shard_map/psum | solution.py:163
  436.4 1.6 multiply_reduce_fusion.1
  438.0 0.0 copy-done.3
  438.1 0.3 abs_reduce_fusion
  438.4 0.4 convolution_convert_fusion
  438.8 0.7 reshape.170
  439.4 0.8 fusion.27
  (19 shorter events, 0.1 us)
Async XLA Ops:
  7.2 235.6 %copy-start = (bf16[32,7168]{1,0:T(8,128)(2,1)S(1)}, bf16[32,7168]{1,0:T(8,128)(2,1)}, u32[]{:S(2)}) copy-start(bf16[32,7168]{1,0:T(8,128)(2,1)} %param.13) | copy-start | bytes 1376260
  7.2 102.7 %all-gather.7.cloned.1.call-start = ((), (), s32[]{:S(2)}) async-start(), calls=%async_computation.4 | async-start | bytes 2641920 | tf_op jit(solution)/shard_map/all_gather | solution.py:110
  8.0 223.7 %all-gather.5.cloned.1.call-start = ((), (), s32[]{:S(2)}) async-start(), calls=%async_computation.2 | async-start | bytes 2113536 | tf_op jit(solution)/shard_map/all_gather | solution.py:27
  121.6 5.2 %copy-start.4 = (s32[40,8]{0,1:T(8,128)S(1)}, s32[40,8]{0,1:T(8,128)}, u32[]{:S(2)}) copy-start(s32[40,8]{0,1:T(8,128)} %param.16) | copy-start | bytes 3844
  140.7 11.2 %copy-start.5 = (bf16[40,56]{1,0:T(8,128)(2,1)S(1)}, bf16[40,56]{1,0:T(8,128)(2,1)}, u32[]{:S(2)}) copy-start(bf16[40,56]{1,0:T(8,128)(2,1)} %param.14) | copy-start | bytes 13444
  140.7 11.2 %copy-start.7 = (bf16[56]{0:T(256)(128)(2,1)S(1)}, bf16[56]{0:T(256)(128)(2,1)}, u32[]{:S(2)}) copy-start(bf16[56]{0:T(256)(128)(2,1)} %param.15) | copy-start | bytes 340
  140.7 94.5 %all-to-all-start.1 = ((bf16[64,2,1,40,128]{4,1,3,2,0:T(2,128)(2,1)}), bf16[64,2,1,40,128]{4,1,3,2,0:T(2,128)(2,1)S(1)}, u32[]{:S(2)}, u32[]{:S(2)}) async-start(bf16[64,2,1,40,128]{4,1,3,2,0:T(2,128)(2,1)} %copy.74), calls=%async_computation.1 | async-start | bytes 2621440 | tf_op jit(solution)/shard_map/all_to_all | solution.py:47
  151.4 285.0 %all-reduce.2.cloned.1.call-start = ((), (), s32[]{:S(2)}) async-start(), calls=%async_computation.3 | async-start | bytes 2293760 | tf_op jit(solution)/shard_map/psum | solution.py:163
  231.7 2.2 copy-start.1
  235.2 3.3 copy-start.8
  238.8 1.3 collective-permute-start
  240.1 2.6 collective-permute-start.1
  241.2 3.0 copy-start.6
  241.2 195.2 %copy-start.2 = (bf16[7168,41]{0,1:T(8,128)(2,1)S(1)}, bf16[7168,41]{0,1:T(8,128)(2,1)}, u32[]{:S(2)}) copy-start(bf16[7168,41]{0,1:T(8,128)(2,1)} %reshape.176) | copy-start | bytes 1763332
  436.4 1.6 copy-start.3
Sparse Core Ops, SparseCore 0:
  10.7 99.1 all-gather.6
  127.0 97.7 all-gather.4
  244.3 192.0 all-reduce.1
where the time goes:
time: 447 us
  waiting for transfers between devices  296 us (66%)
  blocking collectives  80 us (18%)
  local copies, waits for them, and re-layouts  22 us (5%)
  between operations  14 us (3%)
  starting transfers between devices  12.3 us (3%)
  matrix products  12 us (3%)
  other arithmetic  11 us (2%)
    psum x1, waiting for transfers between devices, per_device(): attn_rows = lax.psum(partial_out, KV)  191 us
    all_gather x1, waiting for transfers between devices, per_device(): lax.all_gather(queries, KV, axis=1, tiled=True)  101 us
    all_gather x1, blocking collectives, gather_turned(): result = lax.all_gather(both, axis, axis=0, tiled=True)  75.2 us
    all_to_all x1, starting transfers between devices, moved_by_axis(): result = lax.all_to_all(result, axes[k], k, k, tiled=True)  10.7 us
    unnamed x22, local copies, waits for them, and re-layouts  9.85 us
  transfers between devices with their start and end apart: 6, of which 4 were waited for; matrix products, arithmetic and copies ran while one was open for 4% of the time, Pallas kernels for 0%

commit v1 on v0

v1 whole, which is shorter than its diff:
```python
import functools

import jax
import jax.numpy as jnp
from jax import lax
from jax.experimental import pallas as pl
from jax.experimental.pallas import tpu as pltpu
from jax.sharding import Mesh
from jax.sharding import PartitionSpec as P

H = 32
LAT = 512
ROPE = 64
VD = 128
TOPK = 8
CAP = 2
SIDE = 8
QUARTERS = 4
ROWS = 24
KV = ("kv_0", "kv_1", "kv_2")
GROUPS_KV = ("groups", "kv_0", "kv_1", "kv_2")
MESH = pl.DeviceIdType.MESH
F32 = jnp.float32
BF16 = jnp.bfloat16

score_scale = 192.0 ** (-0.5)
masked_score = -1e30
small_eps = 1e-06

Q1, Q2, QD, O1, ML1, ML2, O2, A1, A2, A3 = range(10)
D_VU, D_RG, D_W, D_O, D_ML, D_F, D_X, D_V = range(8)


def lanes(shape):
    return lax.broadcasted_iota(jnp.int32, shape, len(shape) - 1)


def sublanes(shape):
    return lax.broadcasted_iota(jnp.int32, shape, len(shape) - 2)


def loop(count, body):
    def step(i, carry):
        body(i)
        return carry

    lax.fori_loop(0, count, step, 0)


def far_first(i):
    return SIDE // 2 + (1 - 2 * lax.rem(i, 2)) * lax.div(i + 1, 2)


def kernel(
    q_in, cache_in, ctx, vu_in, op_in, rg_in, ids_in, gate_in,
    disp_out, scale_out, gate_out,
    qraw, ext, qb, qa, cache, s0, r0, ml0, rml0, ow, mlw, s1, r1, ml1, rml1,
    ml2, rml2, fac, acc, ab, s2, r2, vu, vs, vr, rg, ta, tb, lhs, w,
    s3, r3, s4, r4, rf, ids, gate, pt, pick, y, fs, fr, xs, xr,
    loc, ssem, rsem, dsend, drecv,
):
    g = lax.axis_index("groups")
    yy = lax.axis_index("kv_0")
    xx = lax.axis_index("kv_1")
    c = lax.axis_index("kv_2")
    chip = yy * SIDE + xx
    dev = chip * 2 + c
    a = xx + c * (yy - xx)
    b = yy + c * (xx - yy)
    half_x = lax.rem(xx, 2)
    seqs, ctx_dev = cache.shape[0], cache.shape[1]
    half = seqs // 2
    width = w.shape[2]
    tiles = width // 128
    cols = SIDE * width

    def first(p):
        return (g, yy + c * (p - yy), xx + (1 - c) * (p - xx), c)

    def second(p):
        return (g, yy + (1 - c) * (p - yy), xx + c * (p - xx), c)

    partner = (g, yy, xx, 1 - c)
    neighbour = (g, yy, xx + 1 - 2 * half_x, c)

    def rcopy(src, dst, phase, to, frm, device):
        return pltpu.make_async_remote_copy(
            src_ref=src, dst_ref=dst, send_sem=ssem.at[phase, to], recv_sem=rsem.at[phase, frm],
            device_id=device, device_id_type=MESH,
        )

    def dcopy(src, dst, which, device):
        return pltpu.make_async_remote_copy(
            src_ref=src, dst_ref=dst, send_sem=dsend.at[which], recv_sem=drecv.at[which],
            device_id=device, device_id_type=MESH,
        )

    def peers(me, body):
        def one(i):
            body(lax.rem(me + far_first(i), SIDE))

        loop(SIDE - 1, one)

    def local(src, dst, k):
        return pltpu.make_async_copy(src, dst, loc.at[k])

    w_row = pl.multiple_of(half_x * 64 + c * 32, 32)
    q_load = local(q_in, qraw, 0)
    q_load.start()
    small = [
        local(vu_in, vu.at[c], 1),
        local(rg_in, rg.at[c], 2),
        local(ids_in, ids, 3),
        local(gate_in, gate, 4),
    ]
    for copy in small:
        copy.start()
    w_loads = [
        local(op_in.at[:, pl.ds(p * width, width)], w.at[p, pl.ds(w_row, 32), :], 5 + p)
        for p in range(SIDE)
    ]
    for copy in w_loads:
        copy.start()
    parts = 8
    each = seqs // parts
    k_loads = [
        local(cache_in.at[pl.ds(each * p, each)], cache.at[pl.ds(each * p, each)], 13 + p)
        for p in range(parts)
    ]
    for copy in k_loads:
        copy.start()

    barrier = pltpu.get_barrier_semaphore()
    pl.semaphore_signal(barrier, inc=1, device_id=partner, device_id_type=MESH)

    def greet(p):
        pl.semaphore_signal(barrier, inc=1, device_id=first(p), device_id_type=MESH)

    def greet_second(p):
        pl.semaphore_signal(barrier, inc=1, device_id=second(p), device_id_type=MESH)

    peers(a, greet)
    peers(b, greet_second)

    ext[...] = jnp.zeros(ext.shape, F32)
    q_load.wait()
    quarter = half_x * 2 + c
    ext[:, 0:16] = qraw[:, 128:144].astype(F32)
    main = pltpu.roll(qraw[:, 0:128].astype(F32), quarter * 16, 1)
    extra = jnp.zeros((8, 128), F32)
    for k in range(seqs // 8):
        extra = extra + pltpu.roll(ext[8 * k : 8 * k + 8, :], lax.rem(quarter + k, 8) * 16, 1)
    qb[c, b, a] = jnp.concatenate([main, extra], axis=0).astype(BF16)

    pl.semaphore_wait(barrier, 2 * (SIDE - 1) + 1)

    def q1(p):
        return rcopy(qb.at[c, b, a], qb.at[c, b, a], Q1, p, a, first(p))

    def q1_from(p):
        return rcopy(qb.at[c, b, p], qb.at[c, b, p], Q1, p, p, first(p))

    def q2(p):
        return rcopy(qb.at[c, b], qb.at[c, b], Q2, p, b, second(p))

    def q2_from(p):
        return rcopy(qb.at[c, p], qb.at[c, p], Q2, p, p, second(p))

    def qd(p):
        return rcopy(qb.at[c, p], qb.at[c, p], QD, p, p, partner)

    def qd_from(p):
        return rcopy(qb.at[1 - c, p], qb.at[1 - c, p], QD, p, p, partner)

    peers(a, lambda p: q1(p).start())

    for copy in small:
        copy.wait()
    for copy in w_loads:
        copy.wait()
    w_rows = w.at[:, pl.ds(w_row, 32), :]
    to_partner = [
        dcopy(vu.at[c], vu.at[c], D_VU, partner),
        dcopy(rg.at[c], rg.at[c], D_RG, partner),
        dcopy(w_rows, w_rows, D_W, partner),
    ]
    for copy in to_partner:
        copy.start()

    peers(a, lambda p: q1_from(p).wait_recv())
    peers(b, lambda p: q2(p).start())
    qd(b).start()

    for ref in (ml0, mlw, ab, ta, tb, pt):
        ref[...] = jnp.zeros(ref.shape, F32)
    idle_row = pl.multiple_of((1 - half_x) * 64, 64)

    def fill(p):
        w[p, pl.ds(idle_row, 64), :] = jnp.zeros((64, width), BF16)

        def block(k):
            start = pl.multiple_of(k * 16, 16)
            row = start + sublanes((16, width))
            column = p * width + lanes((16, width))
            target = chip * 112 + lax.rem(row, 64) + 56 * lax.div(row, 64)
            hit = jnp.where((column == target) & (lax.rem(row, 64) < 56), 1.0, 0.0)
            w[p, pl.ds(pl.multiple_of(128 + start, 16), 16), :] = hit.astype(BF16)

        loop(8, block)

    loop(SIDE, fill)

    idv = ids[...]
    gatev = gate[...]
    lane_s = lanes((seqs, 128))
    hits = jnp.zeros((seqs, 128), F32)
    hit_cols = []
    gates = []
    for j in range(4):
        expert = (dev if j < 2 else chip * 2 + 1 - c) * 2 + j % 2
        same = idv == expert
        hit = jnp.sum(jnp.where(same, 1.0, 0.0), axis=1, keepdims=True)
        hit_cols.append(hit)
        gates.append(jnp.sum(jnp.where(same, gatev, 0.0), axis=1, keepdims=True))
        hits = jnp.where(lane_s == j, hit, hits)
    lower = jnp.where(lanes((seqs, seqs)) < sublanes((seqs, seqs)), 1.0, 0.0)
    rank = jnp.dot(lower.astype(BF16), hits.astype(BF16), preferred_element_type=F32)
    table = jnp.zeros((seqs, 128), F32)
    gate_slots = jnp.zeros((2, CAP), F32)
    for j in range(4):
        for k in range(CAP):
            col = jnp.where(rank[:, j : j + 1] == float(k), hit_cols[j], 0.0)
            table = jnp.where(lane_s == (j // 2) * 8 + (j % 2) * CAP + k, col, table)
            if j < 2:
                total = jnp.sum(col * gates[j], axis=0, keepdims=True)
                here = (sublanes((2, CAP)) == j) & (lanes((2, CAP)) == k)
                gate_slots = jnp.where(here, total, gate_slots)
    gate_out[...] = gate_slots
    pt[0:seqs, :] = table
    own = jnp.where(c == 0, pt[0:ROWS, :], pt[half : half + ROWS, :])
    own = jnp.where(sublanes((ROWS, 128)) < half, own, 0.0)
    turned = jnp.concatenate([own, jnp.zeros((128 - ROWS, 128), F32)], axis=0).T
    pick[...] = turned[0:16, :]

    for copy in to_partner[:2]:
        copy.wait_recv()
    ta[:, 0:56] = rg[0].astype(F32)
    tb[:, 0:56] = rg[1].astype(F32)
    both = ta[...] + pltpu.roll(tb[...], 64, 1)
    ta[...] = both
    row = sublanes((ROWS, 128))
    mine = jnp.where(c == 0, ta[0:ROWS, :], ta[half : half + ROWS, :])
    gain_row = jnp.broadcast_to(ta[seqs : seqs + 1, :], (ROWS, 128))
    lhs[...] = jnp.where(row < half, mine, jnp.where(row == half, gain_row, 0.0))

    def pass_on(p):
        q2_from(p).wait_recv()
        qd(p).start()

    peers(b, pass_on)
    loop(SIDE, lambda p: qd_from(p).wait_recv())

    lane = lanes((seqs, 128))

    def assemble(h):
        hy = lax.div(h, 4)
        hg = lax.rem(h, 4)
        m = [
            qb[0, hy, 2 * hg].astype(F32),
            qb[1, 2 * hg, hy].astype(F32),
            qb[0, hy, 2 * hg + 1].astype(F32),
            qb[1, 2 * hg + 1, hy].astype(F32),
        ]
        lane8 = lanes((8, 128))
        extras = []
        for k in range(seqs // 8):
            picked = m[0][seqs:]
            for i in range(1, QUARTERS):
                picked = jnp.where(lax.div(lane8, 16) == (k + i) % 8, m[i][seqs:], picked)
            extras.append(pltpu.roll(picked, (128 - 16 * k) % 128, 1))
        e = jnp.concatenate(extras, axis=0)
        m = [v[:seqs] for v in m]
        whole = [
            m[0],
            jnp.where(lane < 16, e, m[1]),
            jnp.where(lane < 16, m[1], jnp.where(lane < 32, e, m[2])),
            jnp.where(lane < 32, m[2], jnp.where(lane < 48, e, m[3])),
            jnp.where(lane < 48, m[3], e),
        ]
        for t in range(5):
            qa[pl.ds(pl.multiple_of((h * 5 + t) * seqs, 8), seqs), :] = whole[t]

    loop(H, assemble)

    for copy in k_loads:
        copy.wait()
    position = dev * ctx_dev + lanes((1, ctx_dev))
    pitch = 5 * seqs

    def attend(s, by_column):
        pieces = []
        for t in range(5):
            groups = []
            for k in range(4):
                if by_column:
                    start, stride = k * pitch, 4 * pitch
                else:
                    start, stride = 8 * k * pitch, pitch
                groups.append(qa[pl.ds(start + t * seqs + s, 8, stride=stride), :])
            pieces.append(jnp.concatenate(groups, axis=0).astype(BF16))
        q = jnp.concatenate(pieces, axis=1)[:, : LAT + ROPE]
        scores = lax.dot_general(
            q, cache[s], (((1,), (1,)), ((), ())), preferred_element_type=F32
        )
        valid = position < ctx[s]
        scores = jnp.where(valid, scores * score_scale, masked_score)
        top = jnp.max(scores, axis=1, keepdims=True)
        weights = jnp.where(valid, jnp.exp(scores - top), 0.0)
        total = jnp.sum(weights, axis=1, keepdims=True)
        out = jnp.dot(weights.astype(BF16), cache[s, :, 0:LAT], preferred_element_type=F32)
        return top, total, out

    lane8 = lanes((8, 128))

    def note(ml, p, k, top, total):
        ml[p] = jnp.where(lane8 == k, top, jnp.where(lane8 == 64 + k, total, ml[p]))

    def by_column(dst, ml):
        def body(i):
            for u in range(4):
                s = i * 4 + u
                top, total, out = attend(s, True)
                for k in range(4):
                    rows = slice(8 * k, 8 * k + 8)
                    for d in range(2):
                        lo = out[rows, 256 * d : 256 * d + 128]
                        hi = out[rows, 256 * d + 128 : 256 * d + 256]
                        dst[2 * k + d, s] = jnp.concatenate([lo, hi], axis=0).astype(dst.dtype)
                        note(ml, 2 * k + d, s, top[rows], total[rows])

        loop(half // 4, body)

    def by_row(dst, ml):
        low = sublanes((8, 128)) < 4

        def merge(u, v, top_half):
            if top_half:
                return jnp.where(low, u, pltpu.roll(v, 4, 0))
            return jnp.where(low, pltpu.roll(u, 4, 0), v)

        def body(i):
            for u in range(2):
                pair = i * 2 + u
                t0, l0, o0 = attend(half + 2 * pair, False)
                t1, l1, o1 = attend(half + 2 * pair + 1, False)
                for k in range(4):
                    rows = slice(8 * k, 8 * k + 8)
                    wide = (8, 128)
                    for d in range(2):
                        top = merge(
                            jnp.broadcast_to(t0[rows], wide), jnp.broadcast_to(t1[rows], wide), d == 0
                        )
                        total = merge(
                            jnp.broadcast_to(l0[rows], wide), jnp.broadcast_to(l1[rows], wide), d == 0
                        )
                        p = 2 * k + d
                        for e in range(2):
                            blocks = [
                                merge(
                                    o0[rows, 128 * t : 128 * t + 128],
                                    o1[rows, 128 * t : 128 * t + 128],
                                    d == 0,
                                )
                                for t in (2 * e, 2 * e + 1)
                            ]
                            index = 2 * pair + e
                            dst[p, index] = jnp.concatenate(blocks, axis=0).astype(dst.dtype)
                            note(ml, p, index, top, total)

        loop(half // 4, body)

    o_partner = dcopy(s0, r0, D_O, partner)
    ml_partner = dcopy(ml0, rml0, D_ML, partner)

    @pl.when(c == 0)
    def _():
        by_row(s0, ml0)

    @pl.when(c == 1)
    def _():
        by_column(s0, ml0)

    ml_partner.start()
    o_partner.start()

    @pl.when(c == 0)
    def _():
        by_column(ow, mlw)

    @pl.when(c == 1)
    def _():
        by_row(ow, mlw)

    ml_partner.wait_recv()

    def mlsend(p):
        return rcopy(ml1.at[p], rml1.at[a], ML1, p, a, first(p))

    def ml_from(p):
        return rcopy(ml1.at[p], rml1.at[p], ML1, p, p, first(p))

    def osend(p):
        return rcopy(s1.at[p], r1.at[a], O1, p, a, first(p))

    def o_from(p):
        return rcopy(s1.at[p], r1.at[p], O1, p, p, first(p))

    def chip_max(p):
        here, there = mlw[p], rml0[p]
        top = jnp.maximum(here, there)
        total = jnp.exp(here - top) * pltpu.roll(here, 64, 1)
        total = total + jnp.exp(there - top) * pltpu.roll(there, 64, 1)
        ml1[p] = jnp.where(lane8 < 64, top, pltpu.roll(total, 64, 1))

    loop(SIDE, chip_max)
    peers(a, lambda p: mlsend(p).start())
    o_partner.wait_recv()

    def chip_sum(p):
        top = ml1[p]
        f_here = jnp.exp(mlw[p] - top)
        f_there = jnp.exp(rml0[p] - top)
        for k in range(half):
            fh = jnp.broadcast_to(f_here[:, k : k + 1], (8, 128))
            ft = jnp.broadcast_to(f_there[:, k : k + 1], (8, 128))
            fh = jnp.concatenate([fh, fh], axis=0)
            ft = jnp.concatenate([ft, ft], axis=0)
            s1[p, k] = (fh * ow[p, k] + ft * r0[p, k].astype(F32)).astype(BF16)

    def chip_send(p):
        chip_sum(p)
        osend(p).start()

    peers(a, chip_send)
    chip_sum(a)

    peers(a, lambda p: ml_from(p).wait_recv())
    rml1[a] = ml1[a]
    top = rml1[0]
    for p in range(1, SIDE):
        top = jnp.maximum(top, rml1[p])
    total = jnp.zeros((8, 128), F32)
    for p in range(SIDE):
        total = total + jnp.exp(rml1[p] - top) * pltpu.roll(rml1[p], 64, 1)
    packed = jnp.where(lane8 < 64, top, pltpu.roll(total, 64, 1))
    ml2[...] = packed

    def ml2_send(p):
        return rcopy(ml2, rml2.at[b], ML2, p, b, second(p))

    def ml2_from(p):
        return rcopy(ml2, rml2.at[p], ML2, p, p, second(p))

    peers(b, lambda p: ml2_send(p).start())
    peers(b, lambda p: ml2_from(p).wait_recv())
    rml2[b] = packed
    top = rml2[0]
    for p in range(1, SIDE):
        top = jnp.maximum(top, rml2[p])
    total = jnp.zeros((8, 128), F32)
    for p in range(SIDE):
        total = total + jnp.exp(rml2[p] - top) * pltpu.roll(rml2[p], 64, 1)
    for p in range(SIDE):
        fac[p] = jnp.exp(rml1[p] - top) / total

    def add(block, p, fresh):
        f = fac[p]
        for k in range(half):
            fk = jnp.broadcast_to(f[:, k : k + 1], (8, 128))
            term = jnp.concatenate([fk, fk], axis=0) * block[k].astype(F32)
            acc[k] = term if fresh else acc[k] + term

    add(s1.at[a], a, True)

    def take(p):
        o_from(p).wait_recv()
        add(r1.at[p], p, False)

    peers(a, take)

    @pl.when(c == 0)
    def _():
        for k in range(half):
            for d in range(2):
                ab[d * 192 + k * 8 : d * 192 + k * 8 + 8, :] = acc[k, 8 * d : 8 * d + 8, :]
        for j in range(SIDE):
            s2[j] = jnp.concatenate(
                [ab[pl.ds(d * 192 + j, ROWS, stride=8), :] for d in range(2)], axis=0
            ).astype(BF16)

    @pl.when(c == 1)
    def _():
        for k in range(half):
            for d in range(2):
                base = ((k % 2) * 2 + d) * 96 + (k // 2) * 8
                ab[base : base + 8, :] = acc[k, 8 * d : 8 * d + 8, :]
        for j in range(SIDE):
            s2[j] = jnp.concatenate(
                [ab[pl.ds(((j % 2) * 2 + d) * 96 + j // 2, ROWS, stride=4), :] for d in range(2)],
                axis=0,
            ).astype(BF16)

    def o2_send(p):
        return rcopy(s2.at[p], r2.at[b], O2, p, b, second(p))

    def o2_from(p):
        return rcopy(s2.at[p], r2.at[p], O2, p, p, second(p))

    peers(b, lambda p: o2_send(p).start())
    peers(b, lambda p: o2_from(p).wait_recv())
    r2[b] = s2[b]
    merged = r2[0].astype(F32)
    for p in range(1, SIDE):
        merged = merged + r2[p].astype(F32)

    part = jnp.zeros((ROWS, VD), F32)
    for k in range(2):
        block = merged[ROWS * k : ROWS * (k + 1)]
        high = block.astype(BF16)
        low = (block - high.astype(F32)).astype(BF16)
        part = part + jnp.dot(high, vu[k], preferred_element_type=F32)
        part = part + jnp.dot(low, vu[k], preferred_element_type=F32)
    vs[...] = part
    swap = dcopy(vs, vr, D_V, neighbour)
    swap.start()
    to_partner[2].wait_recv()
    swap.wait_recv()
    left = jnp.concatenate([(part + vr[...]).astype(BF16), lhs[...].astype(BF16)], axis=1)

    def a1_send(p):
        return rcopy(s3.at[p], r3.at[a], A1, p, a, first(p))

    def a1_from(p):
        return rcopy(s3.at[p], r3.at[p], A1, p, p, first(p))

    def a2_send(p):
        return rcopy(s4, r4.at[b], A2, p, b, second(p))

    def a2_from(p):
        return rcopy(s4, r4.at[p], A2, p, p, second(p))

    def a3_send(p):
        return rcopy(rf.at[a], rf.at[a], A3, p, a, first(p))

    def a3_from(p):
        return rcopy(rf.at[p], rf.at[p], A3, p, p, first(p))

    def project(p):
        out = jnp.dot(left, w[p], preferred_element_type=F32)
        blocks = [out[:, 128 * t : 128 * t + 128] for t in range(tiles)]
        blocks.append(jnp.zeros((8, 128), F32))
        s3[p] = jnp.concatenate(blocks, axis=0).astype(BF16)

    def project_send(p):
        project(p)
        a1_send(p).start()

    peers(a, project_send)
    project(a)
    peers(a, lambda p: a1_from(p).wait_recv())
    r3[a] = s3[a]
    total = r3[0].astype(F32)
    for p in range(1, SIDE):
        total = total + r3[p].astype(F32)
    s4[...] = total.astype(BF16)
    peers(b, lambda p: a2_send(p).start())
    peers(b, lambda p: a2_from(p).wait_recv())
    r4[b] = s4[...]
    total = r4[0].astype(F32)
    for p in range(1, SIDE):
        total = total + r4[p].astype(F32)
    rf[a] = total.astype(BF16)
    peers(a, lambda p: a3_send(p).start())
    peers(a, lambda p: a3_from(p).wait_recv())

    choose = pick[...][:, 0:ROWS]
    choose_b = choose.astype(BF16)
    squares = jnp.zeros((ROWS, 128), F32)
    largest = jnp.zeros((ROWS, 128), F32)
    for p in range(SIDE):
        block = rf[p].astype(F32)
        parts_r = [block[ROWS * t : ROWS * (t + 1)] for t in range(tiles)]
        gains = [v[half : half + 1] for v in parts_r]
        for v, gv in zip(parts_r, gains):
            squares = squares + v * v
            largest = jnp.maximum(largest, jnp.abs(v * gv))
        rows = jnp.concatenate(parts_r, axis=1).astype(BF16)
        chosen = jnp.dot(choose_b, rows, preferred_element_type=F32)
        y[p] = chosen * jnp.concatenate(gains, axis=1)
    inverse = lax.rsqrt(jnp.sum(squares, axis=1, keepdims=True) / cols + small_eps)
    peak = inverse * jnp.max(largest, axis=1, keepdims=True) + small_eps
    spread = jnp.concatenate(
        [jnp.broadcast_to(inverse / peak, (ROWS, 128)), jnp.broadcast_to(peak, (ROWS, 128))], axis=1
    )
    slots = jnp.dot(choose, spread, preferred_element_type=F32, precision=lax.Precision.HIGHEST)
    code = jnp.concatenate([slots[:, 0:128]] * tiles, axis=1)
    peaks = slots[:, 128:256]
    xs[...] = peaks[8:16]
    for k in range(SIDE // 2):
        fs[k] = jnp.concatenate(
            [y[2 * k + d, 8:16, :] * code[8:16] for d in range(2)], axis=0
        ).astype(BF16)
    x_partner = dcopy(xs, xr, D_X, partner)
    f_partner = dcopy(fs, fr, D_F, partner)
    x_partner.start()
    f_partner.start()
    x_partner.wait_recv()
    peaks = peaks[0:8] + xr[...]
    scale_slots = jnp.zeros((2, CAP), F32)
    for j in range(2):
        for k in range(CAP):
            here = (sublanes((2, CAP)) == j) & (lanes((2, CAP)) == k)
            r = CAP * j + k
            scale_slots = jnp.where(here, peaks[r : r + 1, 0:1], scale_slots)
    scale_out[...] = scale_slots
    f_partner.wait_recv()
    for k in range(SIDE // 2):
        there = fr[k].astype(F32)
        for d in range(2):
            p = 2 * k + d
            rows = (y[p, 0:8, :] * code[0:8] + there[8 * d : 8 * d + 8]).astype(BF16)
            disp_out[:, pl.ds(p * width, width)] = rows[0:4]

    peers(a, lambda p: q1(p).wait_send())
    peers(b, lambda p: q2(p).wait_send())
    loop(SIDE, lambda p: qd(p).wait_send())
    peers(a, lambda p: mlsend(p).wait_send())
    peers(a, lambda p: osend(p).wait_send())
    peers(b, lambda p: ml2_send(p).wait_send())
    peers(b, lambda p: o2_send(p).wait_send())
    peers(a, lambda p: a1_send(p).wait_send())
    peers(b, lambda p: a2_send(p).wait_send())
    peers(a, lambda p: a3_send(p).wait_send())
    for copy in to_partner + [o_partner, ml_partner, swap, x_partner, f_partner]:
        copy.wait_send()


def per_device(
    queries, latent_cache, context_lengths, value_up, out_proj, residual, norm_gain, expert_ids,
    gate_weights,
):
    seqs, ctx_dev, entry = latent_cache.shape
    half = seqs // 2
    columns = out_proj.shape[1]
    width = columns // SIDE
    piece = residual.shape[1]
    experts = 2
    rows = (width // 128) * ROWS + 8
    rest = jnp.zeros((7, piece), residual.dtype)
    rg = jnp.concatenate([residual, norm_gain[None, :], rest], axis=0)
    any_space = pl.BlockSpec(memory_space=pl.ANY)
    vmem = pl.BlockSpec(memory_space=pltpu.VMEM)
    smem = pl.BlockSpec(memory_space=pltpu.SMEM)
    V = pltpu.VMEM
    chunk = (SIDE, half, 16, 128)
    eights = (SIDE, 8, 128)
    scratch = [
        V(queries.shape, BF16),
        V((seqs, 128), F32),
        V((2, SIDE, SIDE, seqs + 8, 128), BF16),
        V((H * 5 * seqs, 128), F32),
        V(latent_cache.shape, BF16),
        V(chunk, BF16),
        V(chunk, BF16),
        V(eights, F32),
        V(eights, F32),
        V(chunk, F32),
        V(eights, F32),
        V(chunk, BF16),
        V(chunk, BF16),
        V(eights, F32),
        V(eights, F32),
        V((8, 128), F32),
        V(eights, F32),
        V(eights, F32),
        V(chunk[1:], F32),
        V((384, 128), F32),
        V((SIDE, 2 * ROWS, 128), BF16),
        V((SIDE, 2 * ROWS, 128), BF16),
        V((2, 128, VD), BF16),
        V((ROWS, VD), F32),
        V((ROWS, VD), F32),
        V((2, seqs + 8, piece), BF16),
        V((seqs + 8, 128), F32),
        V((seqs + 8, 128), F32),
        V((ROWS, 128), F32),
        V((SIDE, 256, width), BF16),
        V((SIDE, rows, 128), BF16),
        V((SIDE, rows, 128), BF16),
        V((rows, 128), BF16),
        V((SIDE, rows, 128), BF16),
        V((SIDE, rows, 128), BF16),
        V(expert_ids.shape, jnp.int32),
        V(gate_weights.shape, F32),
        V((seqs + 8, 128), F32),
        V((16, 128), F32),
        V((SIDE, 16, width), F32),
        V((SIDE // 2, 16, width), BF16),
        V((SIDE // 2, 16, width), BF16),
        V((8, 128), F32),
        V((8, 128), F32),
        pltpu.SemaphoreType.DMA((24,)),
        pltpu.SemaphoreType.DMA((10, SIDE)),
        pltpu.SemaphoreType.DMA((10, SIDE)),
        pltpu.SemaphoreType.DMA((8,)),
        pltpu.SemaphoreType.DMA((8,)),
    ]
    dispatched, slot_scale, slot_gate = pl.pallas_call(
        kernel,
        out_shape=(
            jax.ShapeDtypeStruct((experts * CAP, columns), BF16),
            jax.ShapeDtypeStruct((experts, CAP), F32),
            jax.ShapeDtypeStruct((experts, CAP), F32),
        ),
        in_specs=[any_space, any_space, smem] + [any_space] * 5,
        out_specs=(vmem, vmem, vmem),
        scratch_shapes=scratch,
        compiler_params=pltpu.CompilerParams(collective_id=0, has_side_effects=True),
    )(queries, latent_cache, context_lengths, value_up, out_proj, rg, expert_ids, gate_weights)
    return dispatched.reshape(experts, CAP, columns), slot_scale, slot_gate


def solution(mesh):
    split = Mesh(
        mesh.devices.reshape(mesh.shape["groups"], SIDE, SIDE, 2),
        ("groups", "kv_0", "kv_1", "kv_2"),
    )
    in_specs = (
        P("groups", KV),
        P("groups", KV, None),
        P("groups"),
        P(KV, None),
        P(KV, None),
        P("groups", KV),
        P(KV),
        P("groups", None),
        P("groups", None),
    )
    out_specs = (P(GROUPS_KV, None, None), P(GROUPS_KV, None), P(GROUPS_KV, None))
    return jax.shard_map(
        per_device, mesh=split, in_specs=in_specs, out_specs=out_specs, check_vma=False
    )
```

time: 447 us -> 120 us (0.27)
  waiting for transfers between devices: 296 us -> 0 us
  Pallas kernels: 0 us -> 102 us
  blocking collectives: 80 us -> 0 us
  between operations: 14 us -> 0.65 us
  starting transfers between devices: 12.3 us -> 0 us
  matrix products: 12 us -> 0 us
  other arithmetic: 11 us -> 1.39 us
  local copies, waits for them, and re-layouts: 22 us -> 15.3 us
    psum x1 -> x0, waiting for transfers between devices: 191 us -> none  [per_device(): attn_rows = lax.psum(partial_out, KV)]
    pallas_call x0 -> x1, Pallas kernels: none -> 102 us  [per_device(): pl.pallas_call(kernel, out_shape=(jax.ShapeDtypeStruct((experts * CAP, co...]
    all_gather x2 -> x0, waiting for transfers between devices: 101 us -> none  [the longest x1 101 us: per_device(): lax.all_gather(queries, KV, axis=1, tiled=True)]
    all_gather x1 -> x0, blocking collectives: 75.2 us -> none  [gather_turned(): result = lax.all_gather(both, axis, axis=0, tiled=True)]
    dot_general x7 -> x0, matrix products: 12 us -> none  [the longest x1 4.44 us: per_device(): jnp.einsum('shc,scl->shl', weights.astype(jnp.bfloat16), latent_cache[:,...]
    all_to_all x1 -> x0, starting transfers between devices: 10.7 us -> none  [moved_by_axis(): result = lax.all_to_all(result, axes[k], k, k, tiled=True)]
    reduce_sum x6 -> x0, other arithmetic: 6.35 us -> none  [the longest x1 3.32 us: per_device(): merged_sum = jnp.sum(pieces * own_scaling[:, :, :, None], axis=0)]
    all_to_all x1 -> x0, blocking collectives: 4.79 us -> none  [moved_by_axis(): result = lax.all_to_all(result, axes[k], k, k, tiled=True)]
  transfers between devices with their start and end apart: 6 -> 0, of which waited for: 4 -> 0; matrix products, arithmetic and copies ran while one was open for 4% -> 0% of each run, Pallas kernels for 0% -> 0%
where the time goes in v1:
time: 120 us; the launch traced here: 119 us
  Pallas kernels  102 us (85%)
  local copies, waits for them, and re-layouts  15.3 us (13%)
  other arithmetic  1.39 us (1%)
    pallas_call x1, Pallas kernels, per_device(): pl.pallas_call(kernel, out_shape=(jax.ShapeDtypeStruct((experts * CAP, co...  102 us
    unnamed x5, local copies, waits for them, and re-layouts  13.7 us

profile of v1, /device:TPU:513, one launch (start us, length us, event | category | flops | bytes accessed | tf_op | source)
XLA Modules:
  0.0 119.0 jit_solution(1256729119315009416)
XLA Ops:
  0.6 0.1 pad.2.clone
  0.7 1.4 %maximum_maximum_fusion.rg_in = bf16[48,56]{1,0:T(8,128)(2,1)} fusion(bf16[1,56]{1,0:T(2,128)(2,1)} %bitcast.1, bf16[40,56]{1,0:T(8,128)(2,1)} %param.14, bf16[48]{0:T(256)(128)(2,1)S(1)} %pad.2.clone), kind=kLoop, calls=%fused_computation | loop fusion | flops 16128 | bytes 10064 | tf_op jit(solution)/shard_map/concatenate | solution.py:660
  2.1 1.4 %copy.13.ids_in = s32[40,8]{1,0:T(8,128)} copy(s32[40,8]{0,1:T(8,128)} %param.16) | data formatting | bytes 2560 | tf_op args[7]
  3.5 1.4 %copy.14.gate_in = f32[40,8]{1,0:T(8,128)} copy(f32[40,8]{0,1:T(8,128)} %param.17) | data formatting | bytes 2560 | tf_op args[8]
  4.8 8.6 %copy.12.cache_in = bf16[40,128,576]{2,1,0:T(8,128)(2,1)} copy(bf16[40,128,576]{1,2,0:T(8,128)(2,1)} %param.10) | data formatting | bytes 11796480 | tf_op args[1]
  13.4 101.7 %shard_map.112 = (bf16[4,7168]{1,0:T(4,128)(2,1)}, f32[2,2]{1,0:T(2,128)}, f32[2,2]{1,0:T(2,128)}) custom-call(bf16[40,144]{1,0:T(8,128)(2,1)} %q_in.1, bf16[40,128,576]{2,1,0:T(8,128)(2,1)} %copy.12.cache_in, s32[40]{0:T(128)} %ctx.1, bf16[128,128]{1,0:T(8,128)(2,1)} %vu_in.1, bf16[32,7168]{1,0:T(8,128)(2,1)} %op_in.1, ...), custom_call_target="tpu_custom_call" | custom-call | tf_op jit(solution)/shard_map/pallas_call | solution.py:718
  115.1 1.5 %reshape.9 = bf16[2,2,7168]{2,1,0:T(2,128)(2,1)} reshape(bf16[4,7168]{1,0:T(4,128)(2,1)} %get-tuple-element.6) | data formatting | bytes 114688 | tf_op jit(solution)/shard_map/reshape | solution.py:730
  116.6 1.2 %copy.17 = f32[2,2]{1,0:T(2,128)} copy(f32[2,2]{1,0:T(2,128)} %get-tuple-element.13) | data formatting | bytes 32
  117.8 1.2 copy.18
  (1 shorter events, 0.0 us)

commit v2 on v1

--- a/solution.py
+++ b/solution.py
@@ -28,7 +28,7 @@
 small_eps = 1e-06
 
 Q1, Q2, QD, O1, ML1, ML2, O2, A1, A2, A3 = range(10)
-D_VU, D_RG, D_W, D_O, D_ML, D_F, D_X, D_V = range(8)
+D_VU, D_RES, D_GAIN, D_W, D_O, D_ML, D_F, D_X, D_V = range(9)
 
 
 def lanes(shape):
@@ -52,10 +52,10 @@
 
 
 def kernel(
-    q_in, cache_in, ctx, vu_in, op_in, rg_in, ids_in, gate_in,
+    q_in, cache_in, ctx, vu_in, op_in, res_in, gain_in, ids_in, gate_in,
     disp_out, scale_out, gate_out,
     qraw, ext, qb, qa, cache, s0, r0, ml0, rml0, ow, mlw, s1, r1, ml1, rml1,
-    ml2, rml2, fac, acc, ab, s2, r2, vu, vs, vr, rg, ta, tb, lhs, w,
+    ml2, rml2, fac, acc, ab, s2, r2, vu, vs, vr, res, gain, ta, tb, lhs, w,
     s3, r3, s4, r4, rf, ids, gate, pt, pick, y, fs, fr, xs, xr,
     loc, ssem, rsem, dsend, drecv,
 ):
@@ -68,7 +68,7 @@
     a = xx + c * (yy - xx)
     b = yy + c * (xx - yy)
     half_x = lax.rem(xx, 2)
-    seqs, ctx_dev = cache.shape[0], cache.shape[1]
+    seqs, ctx_dev = cache.shape[0], cache.shape[2]
     half = seqs // 2
     width = w.shape[2]
     tiles = width // 128
@@ -109,7 +109,8 @@
     q_load.start()
     small = [
         local(vu_in, vu.at[c], 1),
-        local(rg_in, rg.at[c], 2),
+        local(res_in, res.at[c], 2),
+        local(gain_in, gain.at[c], 21),
         local(ids_in, ids, 3),
         local(gate_in, gate, 4),
     ]
@@ -181,7 +182,8 @@
     w_rows = w.at[:, pl.ds(w_row, 32), :]
     to_partner = [
         dcopy(vu.at[c], vu.at[c], D_VU, partner),
-        dcopy(rg.at[c], rg.at[c], D_RG, partner),
+        dcopy(res.at[c], res.at[c], D_RES, partner),
+        dcopy(gain.at[c], gain.at[c], D_GAIN, partner),
         dcopy(w_rows, w_rows, D_W, partner),
     ]
     for copy in to_partner:
@@ -212,40 +214,40 @@
 
     idv = ids[...]
     gatev = gate[...]
-    lane_s = lanes((seqs, 128))
-    hits = jnp.zeros((seqs, 128), F32)
-    hit_cols = []
+    hits = jnp.zeros((8, seqs), F32)
+    hit_rows = []
     gates = []
     for j in range(4):
         expert = (dev if j < 2 else chip * 2 + 1 - c) * 2 + j % 2
         same = idv == expert
-        hit = jnp.sum(jnp.where(same, 1.0, 0.0), axis=1, keepdims=True)
-        hit_cols.append(hit)
-        gates.append(jnp.sum(jnp.where(same, gatev, 0.0), axis=1, keepdims=True))
-        hits = jnp.where(lane_s == j, hit, hits)
-    lower = jnp.where(lanes((seqs, seqs)) < sublanes((seqs, seqs)), 1.0, 0.0)
-    rank = jnp.dot(lower.astype(BF16), hits.astype(BF16), preferred_element_type=F32)
-    table = jnp.zeros((seqs, 128), F32)
+        hit = jnp.sum(jnp.where(same, 1.0, 0.0), axis=0, keepdims=True)
+        hit_rows.append(hit)
+        gates.append(jnp.sum(jnp.where(same, gatev, 0.0), axis=0, keepdims=True))
+        hits = jnp.where(sublanes((8, seqs)) == j, hit, hits)
+    earlier = jnp.where(sublanes((seqs, seqs)) < lanes((seqs, seqs)), 1.0, 0.0)
+    rank = jnp.dot(hits.astype(BF16), earlier.astype(BF16), preferred_element_type=F32)
+    table = jnp.zeros((16, seqs), F32)
     gate_slots = jnp.zeros((2, CAP), F32)
     for j in range(4):
         for k in range(CAP):
-            col = jnp.where(rank[:, j : j + 1] == float(k), hit_cols[j], 0.0)
-            table = jnp.where(lane_s == (j // 2) * 8 + (j % 2) * CAP + k, col, table)
+            chosen = jnp.where(rank[j : j + 1] == float(k), hit_rows[j], 0.0)
+            r = (j // 2) * 8 + (j % 2) * CAP + k
+            table = jnp.where(sublanes((16, seqs)) == r, chosen, table)
             if j < 2:
-                total = jnp.sum(col * gates[j], axis=0, keepdims=True)
+                total = jnp.sum(chosen * gates[j], axis=1, keepdims=True)
                 here = (sublanes((2, CAP)) == j) & (lanes((2, CAP)) == k)
                 gate_slots = jnp.where(here, total, gate_slots)
     gate_out[...] = gate_slots
-    pt[0:seqs, :] = table
-    own = jnp.where(c == 0, pt[0:ROWS, :], pt[half : half + ROWS, :])
-    own = jnp.where(sublanes((ROWS, 128)) < half, own, 0.0)
-    turned = jnp.concatenate([own, jnp.zeros((128 - ROWS, 128), F32)], axis=0).T
-    pick[...] = turned[0:16, :]
-
-    for copy in to_partner[:2]:
+    pt[:, 0:seqs] = table
+    own = jnp.where(c == 0, pt[...], pltpu.roll(pt[...], 128 - half, 1))
+    pick[...] = jnp.where(lanes((16, 128)) < half, own, 0.0)
+
+    for copy in to_partner[:3]:
         copy.wait_recv()
-    ta[:, 0:56] = rg[0].astype(F32)
-    tb[:, 0:56] = rg[1].astype(F32)
+    ta[0:seqs, 0:56] = res[0].astype(F32)
+    tb[0:seqs, 0:56] = res[1].astype(F32)
+    ta[seqs : seqs + 1, 0:56] = gain[0].astype(F32)
+    tb[seqs : seqs + 1, 0:56] = gain[1].astype(F32)
     both = ta[...] + pltpu.roll(tb[...], 64, 1)
     ta[...] = both
     row = sublanes((ROWS, 128))
@@ -309,15 +311,16 @@
                 groups.append(qa[pl.ds(start + t * seqs + s, 8, stride=stride), :])
             pieces.append(jnp.concatenate(groups, axis=0).astype(BF16))
         q = jnp.concatenate(pieces, axis=1)[:, : LAT + ROPE]
-        scores = lax.dot_general(
-            q, cache[s], (((1,), (1,)), ((), ())), preferred_element_type=F32
-        )
+        scores = jnp.dot(q, cache[s], preferred_element_type=F32)
         valid = position < ctx[s]
         scores = jnp.where(valid, scores * score_scale, masked_score)
         top = jnp.max(scores, axis=1, keepdims=True)
         weights = jnp.where(valid, jnp.exp(scores - top), 0.0)
         total = jnp.sum(weights, axis=1, keepdims=True)
-        out = jnp.dot(weights.astype(BF16), cache[s, :, 0:LAT], preferred_element_type=F32)
+        out = lax.dot_general(
+            weights.astype(BF16), cache[s, 0:LAT, :], (((1,), (1,)), ((), ())),
+            preferred_element_type=F32,
+        )
         return top, total, out
 
     lane8 = lanes((8, 128))
@@ -533,7 +536,7 @@
     vs[...] = part
     swap = dcopy(vs, vr, D_V, neighbour)
     swap.start()
-    to_partner[2].wait_recv()
+    to_partner[3].wait_recv()
     swap.wait_recv()
     left = jnp.concatenate([(part + vr[...]).astype(BF16), lhs[...].astype(BF16)], axis=1)
 
@@ -629,7 +632,8 @@
         for d in range(2):
             p = 2 * k + d
             rows = (y[p, 0:8, :] * code[0:8] + there[8 * d : 8 * d + 8]).astype(BF16)
-            disp_out[:, pl.ds(p * width, width)] = rows[0:4]
+            for e in range(2):
+                disp_out[e, :, pl.ds(p * width, width)] = rows[CAP * e : CAP * e + CAP]
 
     peers(a, lambda p: q1(p).wait_send())
     peers(b, lambda p: q2(p).wait_send())
@@ -656,8 +660,6 @@
     piece = residual.shape[1]
     experts = 2
     rows = (width // 128) * ROWS + 8
-    rest = jnp.zeros((7, piece), residual.dtype)
-    rg = jnp.concatenate([residual, norm_gain[None, :], rest], axis=0)
     any_space = pl.BlockSpec(memory_space=pl.ANY)
     vmem = pl.BlockSpec(memory_space=pltpu.VMEM)
     smem = pl.BlockSpec(memory_space=pltpu.SMEM)
@@ -669,7 +671,7 @@
         V((seqs, 128), F32),
         V((2, SIDE, SIDE, seqs + 8, 128), BF16),
         V((H * 5 * seqs, 128), F32),
-        V(latent_cache.shape, BF16),
+        V((seqs, entry, ctx_dev), BF16),
         V(chunk, BF16),
         V(chunk, BF16),
         V(eights, F32),
@@ -690,7 +692,8 @@
         V((2, 128, VD), BF16),
         V((ROWS, VD), F32),
         V((ROWS, VD), F32),
-        V((2, seqs + 8, piece), BF16),
+        V((2, seqs, piece), BF16),
+        V((2, 1, piece), BF16),
         V((seqs + 8, 128), F32),
         V((seqs + 8, 128), F32),
         V((ROWS, 128), F32),
@@ -700,9 +703,9 @@
         V((rows, 128), BF16),
         V((SIDE, rows, 128), BF16),
         V((SIDE, rows, 128), BF16),
-        V(expert_ids.shape, jnp.int32),
-        V(gate_weights.shape, F32),
-        V((seqs + 8, 128), F32),
+        V(expert_ids.shape[::-1], jnp.int32),
+        V(gate_weights.shape[::-1], F32),
+        V((16, 128), F32),
         V((16, 128), F32),
         V((SIDE, 16, width), F32),
         V((SIDE // 2, 16, width), BF16),
@@ -712,22 +715,25 @@
         pltpu.SemaphoreType.DMA((24,)),
         pltpu.SemaphoreType.DMA((10, SIDE)),
         pltpu.SemaphoreType.DMA((10, SIDE)),
-        pltpu.SemaphoreType.DMA((8,)),
-        pltpu.SemaphoreType.DMA((8,)),
+        pltpu.SemaphoreType.DMA((9,)),
+        pltpu.SemaphoreType.DMA((9,)),
     ]
     dispatched, slot_scale, slot_gate = pl.pallas_call(
         kernel,
         out_shape=(
-            jax.ShapeDtypeStruct((experts * CAP, columns), BF16),
+            jax.ShapeDtypeStruct((experts, CAP, columns), BF16),
             jax.ShapeDtypeStruct((experts, CAP), F32),
             jax.ShapeDtypeStruct((experts, CAP), F32),
         ),
-        in_specs=[any_space, any_space, smem] + [any_space] * 5,
+        in_specs=[any_space, any_space, smem] + [any_space] * 6,
         out_specs=(vmem, vmem, vmem),
         scratch_shapes=scratch,
         compiler_params=pltpu.CompilerParams(collective_id=0, has_side_effects=True),
-    )(queries, latent_cache, context_lengths, value_up, out_proj, rg, expert_ids, gate_weights)
-    return dispatched.reshape(experts, CAP, columns), slot_scale, slot_gate
+    )(
+        queries, latent_cache.transpose(0, 2, 1), context_lengths, value_up, out_proj, residual,
+        norm_gain[None, :], expert_ids.T, gate_weights.T,
+    )
+    return dispatched, slot_scale, slot_gate
 
 
 def solution(mesh):

time: 120 us -> 106 us (0.88)
  local copies, waits for them, and re-layouts: 15.3 us -> 3.91 us
  other arithmetic: 1.39 us -> 0 us
    unnamed x5 -> x3, local copies, waits for them, and re-layouts: 13.7 us -> 3.91 us
    reshape x1 -> x0, local copies, waits for them, and re-layouts: 1.47 us -> none  [per_device(): return (dispatched.reshape(experts, CAP, columns), slot_scale, slot_gate)]
    concatenate x1 -> x0, other arithmetic: 1.39 us -> none  [per_device(): rg = jnp.concatenate([residual, norm_gain[None, :], rest], axis=0)]
where the time goes in v2:
time: 106 us; the launch traced here: 105 us
  Pallas kernels  101 us (95%)
  local copies, waits for them, and re-layouts  3.91 us (4%)
    pallas_call x1, Pallas kernels, per_device(): pl.pallas_call(kernel, out_shape=(jax.ShapeDtypeStruct((experts, CAP, col...  101 us
    unnamed x3, local copies, waits for them, and re-layouts  3.91 us

profile of v2, /device:TPU:513, one launch (start us, length us, event | category | flops | bytes accessed | tf_op | source)
XLA Modules:
  0.0 105.4 jit_solution(2610398825376381814)
XLA Ops:
  0.6 100.9 %shard_map.112 = (bf16[2,2,7168]{2,1,0:T(2,128)(2,1)}, f32[2,2]{1,0:T(2,128)}, f32[2,2]{1,0:T(2,128)}) custom-call(bf16[40,144]{1,0:T(8,128)(2,1)} %q_in.1, bf16[40,576,128]{2,1,0:T(8,128)(2,1)} %bitcast.4, s32[40]{0:T(128)} %ctx.1, bf16[128,128]{1,0:T(8,128)(2,1)} %vu_in.1, bf16[32,7168]{1,0:T(8,128)(2,1)} %op_in.1, bf16[40,56]{1,0:T(8,128)(2,1)} %res_in.1, ...), custom_call_target="tpu_custom_call" | custom-call | tf_op jit(solution)/shard_map/pallas_call | solution.py:721
  101.5 1.5 %copy.15 = bf16[2,2,7168]{2,1,0:T(2,128)(2,1)} copy(bf16[2,2,7168]{2,1,0:T(2,128)(2,1)} %get-tuple-element.6) | data formatting | bytes 114688
  103.0 1.2 %copy.16 = f32[2,2]{1,0:T(2,128)} copy(f32[2,2]{1,0:T(2,128)} %get-tuple-element.7) | data formatting | bytes 32
  104.2 1.2 %copy.17 = f32[2,2]{1,0:T(2,128)} copy(f32[2,2]{1,0:T(2,128)} %get-tuple-element.8) | data formatting | bytes 32

commit v3 on v2

--- a/solution.py
+++ b/solution.py
@@ -17,6 +17,8 @@
 SIDE = 8
 QUARTERS = 4
 ROWS = 24
+PITCH = 5 * ROWS
+A_GROUP = QUARTERS * PITCH + 8
 KV = ("kv_0", "kv_1", "kv_2")
 GROUPS_KV = ("groups", "kv_0", "kv_1", "kv_2")
 MESH = pl.DeviceIdType.MESH
@@ -27,8 +29,8 @@
 masked_score = -1e30
 small_eps = 1e-06
 
-Q1, Q2, QD, O1, ML1, ML2, O2, A1, A2, A3 = range(10)
-D_VU, D_RES, D_GAIN, D_W, D_O, D_ML, D_F, D_X, D_V = range(9)
+Q1, QD, O1, O1B, ML1, ML2, O2, A1, A2, A3 = range(10)
+D_VU, D_RES, D_GAIN, D_W, D_O, D_OB, D_ML, D_F, D_X, D_V = range(10)
 
 
 def lanes(shape):
@@ -54,10 +56,10 @@
 def kernel(
     q_in, cache_in, ctx, vu_in, op_in, res_in, gain_in, ids_in, gate_in,
     disp_out, scale_out, gate_out,
-    qraw, ext, qb, qa, cache, s0, r0, ml0, rml0, ow, mlw, s1, r1, ml1, rml1,
-    ml2, rml2, fac, acc, ab, s2, r2, vu, vs, vr, res, gain, ta, tb, lhs, w,
+    qraw, ext, qb, qa, qc, cache, wb, s0, r0, rml0, ow, mlo, s1, r1, ml1, rml1,
+    ml2, rml2, fown, fpar, wown, wpar, acc, ab, s2, r2, vu, vs, vr, res, gain, ta, tb, lhs, w,
     s3, r3, s4, r4, rf, ids, gate, pt, pick, y, fs, fr, xs, xr,
-    loc, ssem, rsem, dsend, drecv,
+    loc, ssem, rsem, qsend, qrecv, dsend, drecv, steps,
 ):
     g = lax.axis_index("groups")
     yy = lax.axis_index("kv_0")
@@ -161,11 +163,15 @@
     def q1_from(p):
         return rcopy(qb.at[c, b, p], qb.at[c, b, p], Q1, p, p, first(p))
 
-    def q2(p):
-        return rcopy(qb.at[c, b], qb.at[c, b], Q2, p, b, second(p))
-
-    def q2_from(p):
-        return rcopy(qb.at[c, p], qb.at[c, p], Q2, p, p, second(p))
+    def q2(slot, source, chunk, to):
+        block = qb.at[c, source, chunk]
+        return pltpu.make_async_remote_copy(
+            src_ref=block, dst_ref=block, send_sem=qsend.at[slot, chunk],
+            recv_sem=qrecv.at[source, chunk], device_id=second(to), device_id_type=MESH,
+        )
+
+    def at(me, distance):
+        return lax.rem(me + distance, SIDE)
 
     def qd(p):
         return rcopy(qb.at[c, p], qb.at[c, p], QD, p, p, partner)
@@ -174,6 +180,42 @@
         return rcopy(qb.at[1 - c, p], qb.at[1 - c, p], QD, p, p, partner)
 
     peers(a, lambda p: q1(p).start())
+
+    def spread(distances):
+        for d in distances:
+            chunk = at(a, d)
+            if d:
+                q1_from(chunk).wait_recv()
+            for e in (2, 6, 1, 7):
+                q2(e, b, chunk, at(b, e)).start()
+
+    def relay(distances):
+        for d in distances:
+            chunk = at(a, d)
+            source = at(b, 6)
+            q2(1, source, chunk, source).wait_recv()
+            q2(3, source, chunk, at(b, 1)).start()
+            if d % 2 == 0:
+                q2(4, source, chunk, at(b, 2)).start()
+            source = at(b, 2)
+            q2(1, source, chunk, source).wait_recv()
+            q2(5, source, chunk, at(b, 7)).start()
+            if d % 2 == 1:
+                q2(0, source, chunk, at(b, 6)).start()
+
+    spread((0,))
+    spread((1, 7))
+    spread((2, 6))
+    relay((0,))
+    spread((3, 5))
+    spread((4,))
+    relay((1, 7))
+    qd(b).start()
+    relay((2, 6))
+    relay((3, 5))
+    relay((4,))
+    qd(at(b, 2)).start()
+    qd(at(b, 6)).start()
 
     for copy in small:
         copy.wait()
@@ -186,15 +228,269 @@
         dcopy(gain.at[c], gain.at[c], D_GAIN, partner),
         dcopy(w_rows, w_rows, D_W, partner),
     ]
-    for copy in to_partner:
+    for copy in to_partner[:3]:
         copy.start()
 
-    peers(a, lambda p: q1_from(p).wait_recv())
-    peers(b, lambda p: q2(p).start())
-    qd(b).start()
-
-    for ref in (ml0, mlw, ab, ta, tb, pt):
+    for ref in (mlo, ab, ta, tb, pt):
         ref[...] = jnp.zeros(ref.shape, F32)
+    for e in (1, 7, 3, 5, 4):
+        source = at(b, e)
+        loop(SIDE, lambda k: q2(1, source, k, source).wait_recv())
+        qd(source).start()
+    to_partner[3].start()
+    loop(SIDE, lambda p: qd_from(p).wait_recv())
+
+    lane = lanes((seqs, 128))
+
+    lane8 = lanes((8, 128))
+
+    def assemble(hy):
+        for hg in range(QUARTERS):
+            m = [
+                qb[0, hy, 2 * hg].astype(F32),
+                qb[1, 2 * hg, hy].astype(F32),
+                qb[0, hy, 2 * hg + 1].astype(F32),
+                qb[1, 2 * hg + 1, hy].astype(F32),
+            ]
+            extras = []
+            for k in range(seqs // 8):
+                picked = m[0][seqs:]
+                for i in range(1, QUARTERS):
+                    picked = jnp.where(lax.div(lane8, 16) == (k + i) % 8, m[i][seqs:], picked)
+                extras.append(pltpu.roll(picked, (128 - 16 * k) % 128, 1))
+            e = jnp.concatenate(extras, axis=0)
+            m = [v[:seqs] for v in m]
+            whole = [
+                m[0],
+                jnp.where(lane < 16, e, m[1]),
+                jnp.where(lane < 16, m[1], jnp.where(lane < 32, e, m[2])),
+                jnp.where(lane < 32, m[2], jnp.where(lane < 48, e, m[3])),
+                jnp.where(lane < 48, m[3], e),
+            ]
+            for t in range(5):
+                rows = pl.multiple_of(hy * A_GROUP + hg * PITCH + t * ROWS, 8)
+                qa[pl.ds(rows, ROWS), :] = whole[t][:ROWS]
+                rows = pl.multiple_of((hy * QUARTERS + hg) * PITCH + t * ROWS, 8)
+                qc[pl.ds(rows, ROWS), :] = whole[t][seqs - ROWS :]
+
+    loop(SIDE, assemble)
+
+    for copy in k_loads:
+        copy.wait()
+    position = dev * ctx_dev + lanes((1, ctx_dev))
+    part_k = half // 2
+
+    def weigh(s, by_column):
+        pieces = []
+        for t in range(5):
+            groups = []
+            for k in range(4):
+                if by_column:
+                    rows = pl.ds(k * PITCH + t * ROWS + s, 8, stride=A_GROUP)
+                    groups.append(qa[rows, :])
+                else:
+                    rows = pl.ds(8 * k * PITCH + t * ROWS + s - (seqs - ROWS), 8, stride=PITCH)
+                    groups.append(qc[rows, :])
+            pieces.append(jnp.concatenate(groups, axis=0).astype(BF16))
+        q = jnp.concatenate(pieces, axis=1)[:, : LAT + ROPE]
+        scores = jnp.dot(q, cache[s], preferred_element_type=F32)
+        valid = position < ctx[s]
+        scores = jnp.where(valid, scores * score_scale, masked_score)
+        top = jnp.max(scores, axis=1, keepdims=True)
+        weights = jnp.where(valid, jnp.exp(scores - top), 0.0)
+        total = jnp.sum(weights, axis=1, keepdims=True)
+        wb[s] = weights.astype(BF16)
+        return top, total
+
+    low = sublanes((8, 128)) < 4
+
+    def merge(u, v, first_rows):
+        if first_rows:
+            return jnp.where(low, u, pltpu.roll(v, 4, 0))
+        return jnp.where(low, pltpu.roll(u, 4, 0), v)
+
+    def put(tile, k, top, total):
+        return jnp.where(lane8 == k, top, jnp.where(lane8 == 64 + k, total, tile))
+
+    def weigh_columns(i):
+        tiles_m = [jnp.zeros((8, 128), F32) for _ in range(4)]
+        for u in range(part_k):
+            s = i * part_k + u
+            top, total = weigh(s, True)
+            for k in range(4):
+                rows = slice(8 * k, 8 * k + 8)
+                tiles_m[k] = put(tiles_m[k], s, top[rows], total[rows])
+        for k in range(4):
+            for d in range(2):
+                mlo[0, 2 * k + d] += tiles_m[k]
+
+    def weigh_rows(i):
+        tiles_m = [jnp.zeros((8, 128), F32) for _ in range(SIDE)]
+        for u in range(part_k // 2):
+            pair = i * (part_k // 2) + u
+            t0, l0 = weigh(half + 2 * pair, False)
+            t1, l1 = weigh(half + 2 * pair + 1, False)
+            for k in range(4):
+                rows = slice(8 * k, 8 * k + 8)
+                wide = [jnp.broadcast_to(v[rows], (8, 128)) for v in (t0, t1, l0, l1)]
+                for d in range(2):
+                    top = merge(wide[0], wide[1], d == 0)
+                    total = merge(wide[2], wide[3], d == 0)
+                    for e in range(2):
+                        tile = tiles_m[2 * k + d]
+                        tiles_m[2 * k + d] = put(tile, 2 * pair + e, top, total)
+        for p in range(SIDE):
+            mlo[1, p] += tiles_m[p]
+
+    loop(2, weigh_columns)
+    loop(2, weigh_rows)
+    ml_partner = dcopy(mlo.at[1 - c], rml0, D_ML, partner)
+    ml_partner.start()
+
+    def attend(s):
+        return lax.dot_general(
+            wb[s], cache[s, 0:LAT, :], (((1,), (1,)), ((), ())), preferred_element_type=F32
+        )
+
+    def by_column(dst, i):
+        for u in range(part_k):
+            out = attend(i * part_k + u)
+            for k in range(4):
+                rows = slice(8 * k, 8 * k + 8)
+                for d in range(2):
+                    lo = out[rows, 256 * d : 256 * d + 128]
+                    hi = out[rows, 256 * d + 128 : 256 * d + 256]
+                    dst[i, 2 * k + d, u] = jnp.concatenate([lo, hi], axis=0).astype(dst.dtype)
+
+    def by_row(dst, i):
+        for u in range(part_k // 2):
+            s = half + i * part_k + 2 * u
+            o0 = attend(s)
+            o1 = attend(s + 1)
+            for k in range(4):
+                rows = slice(8 * k, 8 * k + 8)
+                for d in range(2):
+                    for e in range(2):
+                        blocks = [
+                            merge(
+                                o0[rows, 128 * t : 128 * t + 128],
+                                o1[rows, 128 * t : 128 * t + 128],
+                                d == 0,
+                            )
+                            for t in (2 * e, 2 * e + 1)
+                        ]
+                        dst[i, 2 * k + d, 2 * u + e] = jnp.concatenate(blocks, axis=0).astype(
+                            dst.dtype
+                        )
+
+    def o_partner(i):
+        return dcopy(s0.at[i], r0.at[i], D_O + i, partner)
+
+    def for_partner(i):
+        @pl.when(c == 0)
+        def _():
+            by_row(s0, i)
+
+        @pl.when(c == 1)
+        def _():
+            by_column(s0, i)
+
+        o_partner(i).start()
+
+    loop(2, for_partner)
+
+    ml_partner.wait_recv()
+
+    def mlsend(p):
+        return rcopy(ml1.at[p], rml1.at[a], ML1, p, a, first(p))
+
+    def ml_from(p):
+        return rcopy(ml1.at[p], rml1.at[p], ML1, p, p, first(p))
+
+    def osend(i, p):
+        return rcopy(s1.at[i, p], r1.at[i, a], O1 + i, p, a, first(p))
+
+    def o_from(i, p):
+        return rcopy(s1.at[i, p], r1.at[i, p], O1 + i, p, p, first(p))
+
+    for p in range(SIDE):
+        here, there = mlo[c, p], rml0[p]
+        top = jnp.maximum(here, there)
+        f_here = jnp.exp(here - top)
+        f_there = jnp.exp(there - top)
+        total = f_here * pltpu.roll(here, 64, 1) + f_there * pltpu.roll(there, 64, 1)
+        ml1[p] = jnp.where(lane8 < 64, top, pltpu.roll(total, 64, 1))
+        fown[p] = f_here
+        fpar[p] = f_there
+    peers(a, lambda p: mlsend(p).start())
+
+    def widen(wide, p, f):
+        for k in range(half):
+            wide[p, k] = jnp.broadcast_to(f[:, k : k + 1], (8, 128))
+
+    def twice(f):
+        return jnp.concatenate([f, f], axis=0)
+
+    def widen_both(i):
+        for d in range(2):
+            widen(wown, 2 * i + d, fown[2 * i + d])
+            widen(wpar, 2 * i + d, fpar[2 * i + d])
+
+    loop(SIDE // 2, widen_both)
+
+    def chip_sum(i, p):
+        for k in range(part_k):
+            fh = twice(wown[p, i * part_k + k])
+            ft = twice(wpar[p, i * part_k + k])
+            s1[i, p, k] = (fh * ow[i, p, k] + ft * r0[i, p, k].astype(F32)).astype(BF16)
+
+    def for_self(i):
+        @pl.when(c == 0)
+        def _():
+            by_column(ow, i)
+
+        @pl.when(c == 1)
+        def _():
+            by_row(ow, i)
+
+        o_partner(i).wait_recv()
+
+        def chip_send(p):
+            chip_sum(i, p)
+            osend(i, p).start()
+
+        peers(a, chip_send)
+        chip_sum(i, a)
+
+    loop(2, for_self)
+
+    peers(a, lambda p: ml_from(p).wait_recv())
+    rml1[a] = ml1[a]
+    row_top = rml1[0]
+    for p in range(1, SIDE):
+        row_top = jnp.maximum(row_top, rml1[p])
+    total = jnp.zeros((8, 128), F32)
+    for p in range(SIDE):
+        factor = jnp.exp(rml1[p] - row_top)
+        total = total + factor * pltpu.roll(rml1[p], 64, 1)
+        fown[p] = factor
+    packed = jnp.where(lane8 < 64, row_top, pltpu.roll(total, 64, 1))
+    ml2[...] = packed
+
+    def ml2_send(p):
+        return rcopy(ml2, rml2.at[b], ML2, p, b, second(p))
+
+    def ml2_from(p):
+        return rcopy(ml2, rml2.at[p], ML2, p, p, second(p))
+
+    peers(b, lambda p: ml2_send(p).start())
+
+    def widen_row(i):
+        for d in range(2):
+            widen(wown, 2 * i + d, fown[2 * i + d])
+
+    loop(SIDE // 2, widen_row)
+
     idle_row = pl.multiple_of((1 - half_x) * 64, 64)
 
     def fill(p):
@@ -255,216 +551,22 @@
     gain_row = jnp.broadcast_to(ta[seqs : seqs + 1, :], (ROWS, 128))
     lhs[...] = jnp.where(row < half, mine, jnp.where(row == half, gain_row, 0.0))
 
-    def pass_on(p):
-        q2_from(p).wait_recv()
-        qd(p).start()
-
-    peers(b, pass_on)
-    loop(SIDE, lambda p: qd_from(p).wait_recv())
-
-    lane = lanes((seqs, 128))
-
-    def assemble(h):
-        hy = lax.div(h, 4)
-        hg = lax.rem(h, 4)
-        m = [
-            qb[0, hy, 2 * hg].astype(F32),
-            qb[1, 2 * hg, hy].astype(F32),
-            qb[0, hy, 2 * hg + 1].astype(F32),
-            qb[1, 2 * hg + 1, hy].astype(F32),
-        ]
-        lane8 = lanes((8, 128))
-        extras = []
-        for k in range(seqs // 8):
-            picked = m[0][seqs:]
-            for i in range(1, QUARTERS):
-                picked = jnp.where(lax.div(lane8, 16) == (k + i) % 8, m[i][seqs:], picked)
-            extras.append(pltpu.roll(picked, (128 - 16 * k) % 128, 1))
-        e = jnp.concatenate(extras, axis=0)
-        m = [v[:seqs] for v in m]
-        whole = [
-            m[0],
-            jnp.where(lane < 16, e, m[1]),
-            jnp.where(lane < 16, m[1], jnp.where(lane < 32, e, m[2])),
-            jnp.where(lane < 32, m[2], jnp.where(lane < 48, e, m[3])),
-            jnp.where(lane < 48, m[3], e),
-        ]
-        for t in range(5):
-            qa[pl.ds(pl.multiple_of((h * 5 + t) * seqs, 8), seqs), :] = whole[t]
-
-    loop(H, assemble)
-
-    for copy in k_loads:
-        copy.wait()
-    position = dev * ctx_dev + lanes((1, ctx_dev))
-    pitch = 5 * seqs
-
-    def attend(s, by_column):
-        pieces = []
-        for t in range(5):
-            groups = []
-            for k in range(4):
-                if by_column:
-                    start, stride = k * pitch, 4 * pitch
-                else:
-                    start, stride = 8 * k * pitch, pitch
-                groups.append(qa[pl.ds(start + t * seqs + s, 8, stride=stride), :])
-            pieces.append(jnp.concatenate(groups, axis=0).astype(BF16))
-        q = jnp.concatenate(pieces, axis=1)[:, : LAT + ROPE]
-        scores = jnp.dot(q, cache[s], preferred_element_type=F32)
-        valid = position < ctx[s]
-        scores = jnp.where(valid, scores * score_scale, masked_score)
-        top = jnp.max(scores, axis=1, keepdims=True)
-        weights = jnp.where(valid, jnp.exp(scores - top), 0.0)
-        total = jnp.sum(weights, axis=1, keepdims=True)
-        out = lax.dot_general(
-            weights.astype(BF16), cache[s, 0:LAT, :], (((1,), (1,)), ((), ())),
-            preferred_element_type=F32,
-        )
-        return top, total, out
-
-    lane8 = lanes((8, 128))
-
-    def note(ml, p, k, top, total):
-        ml[p] = jnp.where(lane8 == k, top, jnp.where(lane8 == 64 + k, total, ml[p]))
-
-    def by_column(dst, ml):
-        def body(i):
-            for u in range(4):
-                s = i * 4 + u
-                top, total, out = attend(s, True)
-                for k in range(4):
-                    rows = slice(8 * k, 8 * k + 8)
-                    for d in range(2):
-                        lo = out[rows, 256 * d : 256 * d + 128]
-                        hi = out[rows, 256 * d + 128 : 256 * d + 256]
-                        dst[2 * k + d, s] = jnp.concatenate([lo, hi], axis=0).astype(dst.dtype)
-                        note(ml, 2 * k + d, s, top[rows], total[rows])
-
-        loop(half // 4, body)
-
-    def by_row(dst, ml):
-        low = sublanes((8, 128)) < 4
-
-        def merge(u, v, top_half):
-            if top_half:
-                return jnp.where(low, u, pltpu.roll(v, 4, 0))
-            return jnp.where(low, pltpu.roll(u, 4, 0), v)
-
-        def body(i):
-            for u in range(2):
-                pair = i * 2 + u
-                t0, l0, o0 = attend(half + 2 * pair, False)
-                t1, l1, o1 = attend(half + 2 * pair + 1, False)
-                for k in range(4):
-                    rows = slice(8 * k, 8 * k + 8)
-                    wide = (8, 128)
-                    for d in range(2):
-                        top = merge(
-                            jnp.broadcast_to(t0[rows], wide), jnp.broadcast_to(t1[rows], wide), d == 0
-                        )
-                        total = merge(
-                            jnp.broadcast_to(l0[rows], wide), jnp.broadcast_to(l1[rows], wide), d == 0
-                        )
-                        p = 2 * k + d
-                        for e in range(2):
-                            blocks = [
-                                merge(
-                                    o0[rows, 128 * t : 128 * t + 128],
-                                    o1[rows, 128 * t : 128 * t + 128],
-                                    d == 0,
-                                )
-                                for t in (2 * e, 2 * e + 1)
-                            ]
-                            index = 2 * pair + e
-                            dst[p, index] = jnp.concatenate(blocks, axis=0).astype(dst.dtype)
-                            note(ml, p, index, top, total)
-
-        loop(half // 4, body)
-
-    o_partner = dcopy(s0, r0, D_O, partner)
-    ml_partner = dcopy(ml0, rml0, D_ML, partner)
-
-    @pl.when(c == 0)
-    def _():
-        by_row(s0, ml0)
-
-    @pl.when(c == 1)
-    def _():
-        by_column(s0, ml0)
-
-    ml_partner.start()
-    o_partner.start()
-
-    @pl.when(c == 0)
-    def _():
-        by_column(ow, mlw)
-
-    @pl.when(c == 1)
-    def _():
-        by_row(ow, mlw)
-
-    ml_partner.wait_recv()
-
-    def mlsend(p):
-        return rcopy(ml1.at[p], rml1.at[a], ML1, p, a, first(p))
-
-    def ml_from(p):
-        return rcopy(ml1.at[p], rml1.at[p], ML1, p, p, first(p))
-
-    def osend(p):
-        return rcopy(s1.at[p], r1.at[a], O1, p, a, first(p))
-
-    def o_from(p):
-        return rcopy(s1.at[p], r1.at[p], O1, p, p, first(p))
-
-    def chip_max(p):
-        here, there = mlw[p], rml0[p]
-        top = jnp.maximum(here, there)
-        total = jnp.exp(here - top) * pltpu.roll(here, 64, 1)
-        total = total + jnp.exp(there - top) * pltpu.roll(there, 64, 1)
-        ml1[p] = jnp.where(lane8 < 64, top, pltpu.roll(total, 64, 1))
-
-    loop(SIDE, chip_max)
-    peers(a, lambda p: mlsend(p).start())
-    o_partner.wait_recv()
-
-    def chip_sum(p):
-        top = ml1[p]
-        f_here = jnp.exp(mlw[p] - top)
-        f_there = jnp.exp(rml0[p] - top)
-        for k in range(half):
-            fh = jnp.broadcast_to(f_here[:, k : k + 1], (8, 128))
-            ft = jnp.broadcast_to(f_there[:, k : k + 1], (8, 128))
-            fh = jnp.concatenate([fh, fh], axis=0)
-            ft = jnp.concatenate([ft, ft], axis=0)
-            s1[p, k] = (fh * ow[p, k] + ft * r0[p, k].astype(F32)).astype(BF16)
-
-    def chip_send(p):
-        chip_sum(p)
-        osend(p).start()
-
-    peers(a, chip_send)
-    chip_sum(a)
-
-    peers(a, lambda p: ml_from(p).wait_recv())
-    rml1[a] = ml1[a]
-    top = rml1[0]
-    for p in range(1, SIDE):
-        top = jnp.maximum(top, rml1[p])
-    total = jnp.zeros((8, 128), F32)
-    for p in range(SIDE):
-        total = total + jnp.exp(rml1[p] - top) * pltpu.roll(rml1[p], 64, 1)
-    packed = jnp.where(lane8 < 64, top, pltpu.roll(total, 64, 1))
-    ml2[...] = packed
-
-    def ml2_send(p):
-        return rcopy(ml2, rml2.at[b], ML2, p, b, second(p))
-
-    def ml2_from(p):
-        return rcopy(ml2, rml2.at[p], ML2, p, p, second(p))
-
-    peers(b, lambda p: ml2_send(p).start())
+    def add(block, i, p, fresh):
+        for k in range(part_k):
+            index = i * part_k + k
+            term = twice(wown[p, index]) * block[k].astype(F32)
+            acc[index] = term if fresh else acc[index] + term
+
+    def gather(i):
+        add(s1.at[i, a], i, a, True)
+
+        def take(p):
+            o_from(i, p).wait_recv()
+            add(r1.at[i, p], i, p, False)
+
+        peers(a, take)
+
+    loop(2, gather)
     peers(b, lambda p: ml2_from(p).wait_recv())
     rml2[b] = packed
     top = rml2[0]
@@ -473,23 +575,9 @@
     total = jnp.zeros((8, 128), F32)
     for p in range(SIDE):
         total = total + jnp.exp(rml2[p] - top) * pltpu.roll(rml2[p], 64, 1)
-    for p in range(SIDE):
-        fac[p] = jnp.exp(rml1[p] - top) / total
-
-    def add(block, p, fresh):
-        f = fac[p]
-        for k in range(half):
-            fk = jnp.broadcast_to(f[:, k : k + 1], (8, 128))
-            term = jnp.concatenate([fk, fk], axis=0) * block[k].astype(F32)
-            acc[k] = term if fresh else acc[k] + term
-
-    add(s1.at[a], a, True)
-
-    def take(p):
-        o_from(p).wait_recv()
-        add(r1.at[p], p, False)
-
-    peers(a, take)
+    final = jnp.exp(row_top - top) / total
+    for k in range(half):
+        acc[k] = acc[k] * twice(jnp.broadcast_to(final[:, k : k + 1], (8, 128)))
 
     @pl.when(c == 0)
     def _():
@@ -558,16 +646,22 @@
     def a3_from(p):
         return rcopy(rf.at[p], rf.at[p], A3, p, p, first(p))
 
+    def in_step(k):
+        pl.semaphore_signal(steps.at[k], inc=1, device_id=partner, device_id_type=MESH)
+        pl.semaphore_wait(steps.at[k], 1)
+
     def project(p):
         out = jnp.dot(left, w[p], preferred_element_type=F32)
-        blocks = [out[:, 128 * t : 128 * t + 128] for t in range(tiles)]
-        blocks.append(jnp.zeros((8, 128), F32))
+        blocks = [out[:half, 128 * t : 128 * t + 128] for t in range(tiles)]
+        blocks += [out[half : half + 1, 128 * t : 128 * t + 128] for t in range(tiles)]
+        blocks.append(jnp.zeros((rf.shape[1] - tiles * (half + 1), 128), F32))
         s3[p] = jnp.concatenate(blocks, axis=0).astype(BF16)
 
     def project_send(p):
         project(p)
         a1_send(p).start()
 
+    in_step(0)
     peers(a, project_send)
     project(a)
     peers(a, lambda p: a1_from(p).wait_recv())
@@ -576,24 +670,42 @@
     for p in range(1, SIDE):
         total = total + r3[p].astype(F32)
     s4[...] = total.astype(BF16)
+    in_step(1)
     peers(b, lambda p: a2_send(p).start())
+    peers(a, lambda p: q1(p).wait_send())
+    for d in range(SIDE):
+        chunk = at(a, d)
+        for slot in (1, 2, 3, 5, 6, 7, 4 if d % 2 == 0 else 0):
+            q2(slot, b, chunk, at(b, 1)).wait_send()
+    loop(SIDE, lambda p: qd(p).wait_send())
+    peers(a, lambda p: mlsend(p).wait_send())
+    for i in range(2):
+        peers(a, lambda p: osend(i, p).wait_send())
+        o_partner(i).wait_send()
+    peers(b, lambda p: ml2_send(p).wait_send())
+    peers(b, lambda p: o2_send(p).wait_send())
+    for copy in to_partner + [ml_partner, swap]:
+        copy.wait_send()
     peers(b, lambda p: a2_from(p).wait_recv())
     r4[b] = s4[...]
     total = r4[0].astype(F32)
     for p in range(1, SIDE):
         total = total + r4[p].astype(F32)
     rf[a] = total.astype(BF16)
+    in_step(2)
     peers(a, lambda p: a3_send(p).start())
+    peers(a, lambda p: a1_send(p).wait_send())
+    peers(b, lambda p: a2_send(p).wait_send())
     peers(a, lambda p: a3_from(p).wait_recv())
 
-    choose = pick[...][:, 0:ROWS]
+    choose = pick[...][:, 0:half]
     choose_b = choose.astype(BF16)
-    squares = jnp.zeros((ROWS, 128), F32)
-    largest = jnp.zeros((ROWS, 128), F32)
+    squares = jnp.zeros((half, 128), F32)
+    largest = jnp.zeros((half, 128), F32)
     for p in range(SIDE):
         block = rf[p].astype(F32)
-        parts_r = [block[ROWS * t : ROWS * (t + 1)] for t in range(tiles)]
-        gains = [v[half : half + 1] for v in parts_r]
+        parts_r = [block[half * t : half * (t + 1)] for t in range(tiles)]
+        gains = [block[half * tiles + t : half * tiles + t + 1] for t in range(tiles)]
         for v, gv in zip(parts_r, gains):
             squares = squares + v * v
             largest = jnp.maximum(largest, jnp.abs(v * gv))
@@ -603,7 +715,7 @@
     inverse = lax.rsqrt(jnp.sum(squares, axis=1, keepdims=True) / cols + small_eps)
     peak = inverse * jnp.max(largest, axis=1, keepdims=True) + small_eps
     spread = jnp.concatenate(
-        [jnp.broadcast_to(inverse / peak, (ROWS, 128)), jnp.broadcast_to(peak, (ROWS, 128))], axis=1
+        [jnp.broadcast_to(inverse / peak, (half, 128)), jnp.broadcast_to(peak, (half, 128))], axis=1
     )
     slots = jnp.dot(choose, spread, preferred_element_type=F32, precision=lax.Precision.HIGHEST)
     code = jnp.concatenate([slots[:, 0:128]] * tiles, axis=1)
@@ -635,18 +747,9 @@
             for e in range(2):
                 disp_out[e, :, pl.ds(p * width, width)] = rows[CAP * e : CAP * e + CAP]
 
-    peers(a, lambda p: q1(p).wait_send())
-    peers(b, lambda p: q2(p).wait_send())
-    loop(SIDE, lambda p: qd(p).wait_send())
-    peers(a, lambda p: mlsend(p).wait_send())
-    peers(a, lambda p: osend(p).wait_send())
-    peers(b, lambda p: ml2_send(p).wait_send())
-    peers(b, lambda p: o2_send(p).wait_send())
-    peers(a, lambda p: a1_send(p).wait_send())
-    peers(b, lambda p: a2_send(p).wait_send())
     peers(a, lambda p: a3_send(p).wait_send())
-    for copy in to_partner + [o_partner, ml_partner, swap, x_partner, f_partner]:
-        copy.wait_send()
+    x_partner.wait_send()
+    f_partner.wait_send()
 
 
 def per_device(
@@ -659,25 +762,26 @@
     width = columns // SIDE
     piece = residual.shape[1]
     experts = 2
-    rows = (width // 128) * ROWS + 8
+    rows = -(-(width // 128) * (half + 1) // 8) * 8
     any_space = pl.BlockSpec(memory_space=pl.ANY)
     vmem = pl.BlockSpec(memory_space=pltpu.VMEM)
     smem = pl.BlockSpec(memory_space=pltpu.SMEM)
     V = pltpu.VMEM
-    chunk = (SIDE, half, 16, 128)
+    chunk = (2, SIDE, half // 2, 16, 128)
     eights = (SIDE, 8, 128)
     scratch = [
         V(queries.shape, BF16),
         V((seqs, 128), F32),
         V((2, SIDE, SIDE, seqs + 8, 128), BF16),
-        V((H * 5 * seqs, 128), F32),
+        V((SIDE * A_GROUP, 128), F32),
+        V((H * PITCH, 128), F32),
         V((seqs, entry, ctx_dev), BF16),
+        V((seqs, H, ctx_dev), BF16),
         V(chunk, BF16),
         V(chunk, BF16),
         V(eights, F32),
-        V(eights, F32),
         V(chunk, F32),
-        V(eights, F32),
+        V((2,) + eights, F32),
         V(chunk, BF16),
         V(chunk, BF16),
         V(eights, F32),
@@ -685,7 +789,10 @@
         V((8, 128), F32),
         V(eights, F32),
         V(eights, F32),
-        V(chunk[1:], F32),
+        V(eights, F32),
+        V((SIDE, half, 8, 128), F32),
+        V((SIDE, half, 8, 128), F32),
+        V((half, 16, 128), F32),
         V((384, 128), F32),
         V((SIDE, 2 * ROWS, 128), BF16),
         V((SIDE, 2 * ROWS, 128), BF16),
@@ -715,8 +822,11 @@
         pltpu.SemaphoreType.DMA((24,)),
         pltpu.SemaphoreType.DMA((10, SIDE)),
         pltpu.SemaphoreType.DMA((10, SIDE)),
-        pltpu.SemaphoreType.DMA((9,)),
-        pltpu.SemaphoreType.DMA((9,)),
+        pltpu.SemaphoreType.DMA((SIDE, SIDE)),
+        pltpu.SemaphoreType.DMA((SIDE, SIDE)),
+        pltpu.SemaphoreType.DMA((10,)),
+        pltpu.SemaphoreType.DMA((10,)),
+        pltpu.SemaphoreType.REGULAR((3,)),
     ]
     dispatched, slot_scale, slot_gate = pl.pallas_call(
         kernel,

time: 106 us -> 92.5 us (0.87)
  Pallas kernels: 101 us -> 87.7 us
    pallas_call x1, Pallas kernels: 101 us -> 87.7 us  [per_device(): pl.pallas_call(kernel, out_shape=(jax.ShapeDtypeStruct((experts, CAP, col...]
where the time goes in v3:
time: 92.5 us; the launch traced here: 92.3 us
  Pallas kernels  87.7 us (95%)
  local copies, waits for them, and re-layouts  3.91 us (4%)
    pallas_call x1, Pallas kernels, per_device(): pl.pallas_call(kernel, out_shape=(jax.ShapeDtypeStruct((experts, CAP, col...  87.7 us
    unnamed x3, local copies, waits for them, and re-layouts  3.91 us

profile of v3, /device:TPU:513, one launch (start us, length us, event | category | flops | bytes accessed | tf_op | source)
XLA Modules:
  0.0 92.3 jit_solution(6481926198585991721)
XLA Ops:
  0.6 87.7 %shard_map.112 = (bf16[2,2,7168]{2,1,0:T(2,128)(2,1)}, f32[2,2]{1,0:T(2,128)}, f32[2,2]{1,0:T(2,128)}) custom-call(bf16[40,144]{1,0:T(8,128)(2,1)} %q_in.1, bf16[40,576,128]{2,1,0:T(8,128)(2,1)} %bitcast.4, s32[40]{0:T(128)} %ctx.1, bf16[128,128]{1,0:T(8,128)(2,1)} %vu_in.1, bf16[32,7168]{1,0:T(8,128)(2,1)} %op_in.1, bf16[40,56]{1,0:T(8,128)(2,1)} %res_in.1, ...), custom_call_target="tpu_custom_call" | custom-call | tf_op jit(solution)/shard_map/pallas_call | solution.py:831
  88.4 1.5 %copy.15 = bf16[2,2,7168]{2,1,0:T(2,128)(2,1)} copy(bf16[2,2,7168]{2,1,0:T(2,128)(2,1)} %get-tuple-element.6) | data formatting | bytes 114688
  89.8 1.2 %copy.16 = f32[2,2]{1,0:T(2,128)} copy(f32[2,2]{1,0:T(2,128)} %get-tuple-element.7) | data formatting | bytes 32
  91.0 1.2 %copy.17 = f32[2,2]{1,0:T(2,128)} copy(f32[2,2]{1,0:T(2,128)} %get-tuple-element.8) | data formatting | bytes 32

commit v4 on v3

--- a/solution.py
+++ b/solution.py
@@ -29,8 +29,8 @@
 masked_score = -1e30
 small_eps = 1e-06
 
-Q1, QD, O1, O1B, ML1, ML2, O2, A1, A2, A3 = range(10)
-D_VU, D_RES, D_GAIN, D_W, D_O, D_OB, D_ML, D_F, D_X, D_V = range(10)
+Q1, Q1B, O1, O1B, ML1, ML2, O2, A1, A2, A3 = range(10)
+D_VU, D_RES, D_GAIN, D_W, D_F, D_X, D_V = range(7)
 
 
 def lanes(shape):
@@ -56,10 +56,10 @@
 def kernel(
     q_in, cache_in, ctx, vu_in, op_in, res_in, gain_in, ids_in, gate_in,
     disp_out, scale_out, gate_out,
-    qraw, ext, qb, qa, qc, cache, wb, s0, r0, rml0, ow, mlo, s1, r1, ml1, rml1,
-    ml2, rml2, fown, fpar, wown, wpar, acc, ab, s2, r2, vu, vs, vr, res, gain, ta, tb, lhs, w,
+    qraw, ext, main, qs, qb, qa, cache, wb, s1, r1, ml1, rml1,
+    ml2, rml2, fown, wown, acc, ab, s2, r2, vu, vs, vr, res, gain, ta, tb, lhs, w,
     s3, r3, s4, r4, rf, ids, gate, pt, pick, y, fs, fr, xs, xr,
-    loc, ssem, rsem, qsend, qrecv, dsend, drecv, steps,
+    loc, ssem, rsem, qsend, qrecv, ksend, krecv, dsend, drecv, steps,
 ):
     g = lax.axis_index("groups")
     yy = lax.axis_index("kv_0")
@@ -70,8 +70,8 @@
     a = xx + c * (yy - xx)
     b = yy + c * (xx - yy)
     half_x = lax.rem(xx, 2)
-    seqs, ctx_dev = cache.shape[0], cache.shape[2]
-    half = seqs // 2
+    half, ctx_dev = cache.shape[1], cache.shape[3]
+    seqs = 2 * half
     width = w.shape[2]
     tiles = width // 128
     cols = SIDE * width
@@ -82,12 +82,16 @@
     def second(p):
         return (g, yy + (1 - c) * (p - yy), xx + c * (p - xx), c)
 
+    def across(p):
+        return (g, yy + (1 - c) * (p - yy), xx + c * (p - xx), 1 - c)
+
     partner = (g, yy, xx, 1 - c)
     neighbour = (g, yy, xx + 1 - 2 * half_x, c)
 
-    def rcopy(src, dst, phase, to, frm, device):
+    def rcopy(src, dst, phase, to, frm, device, recv_phase=None, recv_from=None):
+        recv = (phase, frm) if recv_phase is None else (recv_phase, recv_from)
         return pltpu.make_async_remote_copy(
-            src_ref=src, dst_ref=dst, send_sem=ssem.at[phase, to], recv_sem=rsem.at[phase, frm],
+            src_ref=src, dst_ref=dst, send_sem=ssem.at[phase, to], recv_sem=rsem.at[recv],
             device_id=device, device_id_type=MESH,
         )
 
@@ -112,7 +116,7 @@
     small = [
         local(vu_in, vu.at[c], 1),
         local(res_in, res.at[c], 2),
-        local(gain_in, gain.at[c], 21),
+        local(gain_in, gain.at[c], 23),
         local(ids_in, ids, 3),
         local(gate_in, gate, 4),
     ]
@@ -124,12 +128,29 @@
     ]
     for copy in w_loads:
         copy.start()
-    parts = 8
-    each = seqs // parts
+    parts = ksend.shape[0]
+    each = half // parts
     k_loads = [
-        local(cache_in.at[pl.ds(each * p, each)], cache.at[pl.ds(each * p, each)], 13 + p)
+        local(
+            cache_in.at[pl.ds(c * half + each * p, each)], cache.at[c, pl.ds(each * p, each)], 13 + p
+        )
         for p in range(parts)
     ]
+
+    def k_copy(p):
+        return pltpu.make_async_remote_copy(
+            src_ref=cache_in.at[pl.ds((1 - c) * half + each * p, each)],
+            dst_ref=cache.at[c, pl.ds(each * p, each)],
+            send_sem=ksend.at[p], recv_sem=krecv.at[p], device_id=partner, device_id_type=MESH,
+        )
+
+    def k_from(p):
+        return pltpu.make_async_remote_copy(
+            src_ref=cache_in.at[pl.ds(each * p, each)],
+            dst_ref=cache.at[1 - c, pl.ds(each * p, each)],
+            send_sem=ksend.at[p], recv_sem=krecv.at[p], device_id=partner, device_id_type=MESH,
+        )
+
     for copy in k_loads:
         copy.start()
 
@@ -138,9 +159,12 @@
 
     def greet(p):
         pl.semaphore_signal(barrier, inc=1, device_id=first(p), device_id_type=MESH)
+        y, x = first(p)[1:3]
+        pl.semaphore_signal(barrier, inc=1, device_id=(g, y, x, 1 - c), device_id_type=MESH)
 
     def greet_second(p):
         pl.semaphore_signal(barrier, inc=1, device_id=second(p), device_id_type=MESH)
+        pl.semaphore_signal(barrier, inc=1, device_id=across(p), device_id_type=MESH)
 
     peers(a, greet)
     peers(b, greet_second)
@@ -149,22 +173,36 @@
     q_load.wait()
     quarter = half_x * 2 + c
     ext[:, 0:16] = qraw[:, 128:144].astype(F32)
-    main = pltpu.roll(qraw[:, 0:128].astype(F32), quarter * 16, 1)
-    extra = jnp.zeros((8, 128), F32)
-    for k in range(seqs // 8):
-        extra = extra + pltpu.roll(ext[8 * k : 8 * k + 8, :], lax.rem(quarter + k, 8) * 16, 1)
-    qb[c, b, a] = jnp.concatenate([main, extra], axis=0).astype(BF16)
-
-    pl.semaphore_wait(barrier, 2 * (SIDE - 1) + 1)
+    main[...] = pltpu.roll(qraw[:, 0:128].astype(F32), quarter * 16, 1)
+
+    def chunk_of(base):
+        extra = jnp.zeros((4, 128), F32)
+        for k in range(half // 4):
+            row = base + 4 * k
+            extra = extra + pltpu.roll(ext[row : row + 4, :], lax.rem(quarter + k, 8) * 16, 1)
+        return jnp.concatenate([main[base : base + half, :], extra], axis=0)
+
+    halves = [chunk_of(0), chunk_of(half)]
+    qb[b, a, c] = jnp.where(c == 0, halves[0], halves[1]).astype(BF16)
+    qs[...] = jnp.where(c == 0, halves[1], halves[0]).astype(BF16)
+
+    pl.semaphore_wait(barrier, 4 * (SIDE - 1) + 1)
 
     def q1(p):
-        return rcopy(qb.at[c, b, a], qb.at[c, b, a], Q1, p, a, first(p))
-
-    def q1_from(p):
-        return rcopy(qb.at[c, b, p], qb.at[c, b, p], Q1, p, p, first(p))
+        return rcopy(qb.at[b, a, c], qb.at[b, a, c], Q1, p, 0, first(p), Q1 + c, a)
+
+    def q1_across(p):
+        return rcopy(qs, qb.at[a, b, c], Q1B, p, 0, across(p), Q1 + c, b)
+
+    def q1_from(p, core):
+        return rcopy(qs, qb.at[b, p, core], Q1, p, 0, first(p), Q1 + core, p)
+
+    q1_across(b).start()
+    peers(a, lambda p: q1(p).start())
+    peers(b, lambda p: q1_across(p).start())
 
     def q2(slot, source, chunk, to):
-        block = qb.at[c, source, chunk]
+        block = qb.at[source, chunk]
         return pltpu.make_async_remote_copy(
             src_ref=block, dst_ref=block, send_sem=qsend.at[slot, chunk],
             recv_sem=qrecv.at[source, chunk], device_id=second(to), device_id_type=MESH,
@@ -173,19 +211,12 @@
     def at(me, distance):
         return lax.rem(me + distance, SIDE)
 
-    def qd(p):
-        return rcopy(qb.at[c, p], qb.at[c, p], QD, p, p, partner)
-
-    def qd_from(p):
-        return rcopy(qb.at[1 - c, p], qb.at[1 - c, p], QD, p, p, partner)
-
-    peers(a, lambda p: q1(p).start())
-
     def spread(distances):
         for d in distances:
             chunk = at(a, d)
             if d:
-                q1_from(chunk).wait_recv()
+                q1_from(chunk, c).wait_recv()
+            q1_from(chunk, 1 - c).wait_recv()
             for e in (2, 6, 1, 7):
                 q2(e, b, chunk, at(b, e)).start()
 
@@ -204,18 +235,25 @@
                 q2(0, source, chunk, at(b, 6)).start()
 
     spread((0,))
+    k_copy(0).start()
     spread((1, 7))
+    k_copy(1).start()
     spread((2, 6))
+    k_copy(2).start()
     relay((0,))
+    k_copy(3).start()
     spread((3, 5))
+    k_copy(4).start()
     spread((4,))
+    k_copy(5).start()
     relay((1, 7))
-    qd(b).start()
+    k_copy(6).start()
     relay((2, 6))
+    k_copy(7).start()
     relay((3, 5))
+    k_copy(8).start()
     relay((4,))
-    qd(at(b, 2)).start()
-    qd(at(b, 6)).start()
+    k_copy(9).start()
 
     for copy in small:
         copy.wait()
@@ -231,35 +269,39 @@
     for copy in to_partner[:3]:
         copy.start()
 
-    for ref in (mlo, ab, ta, tb, pt):
+    for ref in (ml1, ab, ta, tb, pt):
         ref[...] = jnp.zeros(ref.shape, F32)
     for e in (1, 7, 3, 5, 4):
         source = at(b, e)
         loop(SIDE, lambda k: q2(1, source, k, source).wait_recv())
-        qd(source).start()
     to_partner[3].start()
-    loop(SIDE, lambda p: qd_from(p).wait_recv())
-
-    lane = lanes((seqs, 128))
-
+
+    lane = lanes((ROWS, 128))
     lane8 = lanes((8, 128))
+    low = sublanes((8, 128)) < 4
 
     def assemble(hy):
         for hg in range(QUARTERS):
-            m = [
-                qb[0, hy, 2 * hg].astype(F32),
-                qb[1, 2 * hg, hy].astype(F32),
-                qb[0, hy, 2 * hg + 1].astype(F32),
-                qb[1, 2 * hg + 1, hy].astype(F32),
-            ]
-            extras = []
-            for k in range(seqs // 8):
-                picked = m[0][seqs:]
+            m = []
+            for e in range(2):
+                x = 2 * hg + e
+                for q in range(2):
+                    m.append(qb[hy + c * (x - hy), x + c * (hy - x), q].astype(F32))
+            turned = []
+            for k in range(half // 4):
+                picked = m[0][16:ROWS]
                 for i in range(1, QUARTERS):
-                    picked = jnp.where(lax.div(lane8, 16) == (k + i) % 8, m[i][seqs:], picked)
-                extras.append(pltpu.roll(picked, (128 - 16 * k) % 128, 1))
-            e = jnp.concatenate(extras, axis=0)
-            m = [v[:seqs] for v in m]
+                    picked = jnp.where(lax.div(lane8, 16) == (k + i) % 8, m[i][16:ROWS], picked)
+                picked = pltpu.roll(picked, (128 - 16 * k) % 128, 1)
+                turned.append(picked if k % 2 else pltpu.roll(picked, 4, 0))
+            e = jnp.concatenate(
+                [
+                    jnp.where(low, turned[0], turned[1]),
+                    jnp.where(low, turned[2], turned[3]),
+                    turned[4],
+                ],
+                axis=0,
+            )
             whole = [
                 m[0],
                 jnp.where(lane < 16, e, m[1]),
@@ -267,17 +309,17 @@
                 jnp.where(lane < 32, m[2], jnp.where(lane < 48, e, m[3])),
                 jnp.where(lane < 48, m[3], e),
             ]
+            base = hy * (A_GROUP - 8 * c) + hg * PITCH
             for t in range(5):
-                rows = pl.multiple_of(hy * A_GROUP + hg * PITCH + t * ROWS, 8)
-                qa[pl.ds(rows, ROWS), :] = whole[t][:ROWS]
-                rows = pl.multiple_of((hy * QUARTERS + hg) * PITCH + t * ROWS, 8)
-                qc[pl.ds(rows, ROWS), :] = whole[t][seqs - ROWS :]
+                qa[pl.ds(pl.multiple_of(base + t * ROWS, 8), ROWS), :] = whole[t]
 
     loop(SIDE, assemble)
 
     for copy in k_loads:
         copy.wait()
-    position = dev * ctx_dev + lanes((1, ctx_dev))
+    for p in range(parts):
+        k_from(p).wait_recv()
+    position = chip * 2 * ctx_dev + lanes((1, 2 * ctx_dev))
     part_k = half // 2
 
     def weigh(s, by_column):
@@ -287,22 +329,20 @@
             for k in range(4):
                 if by_column:
                     rows = pl.ds(k * PITCH + t * ROWS + s, 8, stride=A_GROUP)
-                    groups.append(qa[rows, :])
                 else:
-                    rows = pl.ds(8 * k * PITCH + t * ROWS + s - (seqs - ROWS), 8, stride=PITCH)
-                    groups.append(qc[rows, :])
+                    rows = pl.ds(8 * k * PITCH + t * ROWS + s, 8, stride=PITCH)
+                groups.append(qa[rows, :])
             pieces.append(jnp.concatenate(groups, axis=0).astype(BF16))
         q = jnp.concatenate(pieces, axis=1)[:, : LAT + ROPE]
-        scores = jnp.dot(q, cache[s], preferred_element_type=F32)
-        valid = position < ctx[s]
+        keys = jnp.concatenate([cache[0, s], cache[1, s]], axis=1)
+        scores = jnp.dot(q, keys, preferred_element_type=F32)
+        valid = position < ctx[c * half + s]
         scores = jnp.where(valid, scores * score_scale, masked_score)
         top = jnp.max(scores, axis=1, keepdims=True)
         weights = jnp.where(valid, jnp.exp(scores - top), 0.0)
         total = jnp.sum(weights, axis=1, keepdims=True)
         wb[s] = weights.astype(BF16)
         return top, total
-
-    low = sublanes((8, 128)) < 4
 
     def merge(u, v, first_rows):
         if first_rows:
@@ -322,14 +362,14 @@
                 tiles_m[k] = put(tiles_m[k], s, top[rows], total[rows])
         for k in range(4):
             for d in range(2):
-                mlo[0, 2 * k + d] += tiles_m[k]
+                ml1[2 * k + d] += tiles_m[k]
 
     def weigh_rows(i):
         tiles_m = [jnp.zeros((8, 128), F32) for _ in range(SIDE)]
         for u in range(part_k // 2):
             pair = i * (part_k // 2) + u
-            t0, l0 = weigh(half + 2 * pair, False)
-            t1, l1 = weigh(half + 2 * pair + 1, False)
+            t0, l0 = weigh(2 * pair, False)
+            t1, l1 = weigh(2 * pair + 1, False)
             for k in range(4):
                 rows = slice(8 * k, 8 * k + 8)
                 wide = [jnp.broadcast_to(v[rows], (8, 128)) for v in (t0, t1, l0, l1)]
@@ -340,16 +380,28 @@
                         tile = tiles_m[2 * k + d]
                         tiles_m[2 * k + d] = put(tile, 2 * pair + e, top, total)
         for p in range(SIDE):
-            mlo[1, p] += tiles_m[p]
-
-    loop(2, weigh_columns)
-    loop(2, weigh_rows)
-    ml_partner = dcopy(mlo.at[1 - c], rml0, D_ML, partner)
-    ml_partner.start()
+            ml1[p] += tiles_m[p]
+
+    @pl.when(c == 0)
+    def _():
+        loop(2, weigh_columns)
+
+    @pl.when(c == 1)
+    def _():
+        loop(2, weigh_rows)
+
+    def mlsend(p):
+        return rcopy(ml1.at[p], rml1.at[a], ML1, p, a, first(p))
+
+    def ml_from(p):
+        return rcopy(ml1.at[p], rml1.at[p], ML1, p, p, first(p))
+
+    peers(a, lambda p: mlsend(p).start())
 
     def attend(s):
+        values = jnp.concatenate([cache[0, s, 0:LAT, :], cache[1, s, 0:LAT, :]], axis=1)
         return lax.dot_general(
-            wb[s], cache[s, 0:LAT, :], (((1,), (1,)), ((), ())), preferred_element_type=F32
+            wb[s], values, (((1,), (1,)), ((), ())), preferred_element_type=F32
         )
 
     def by_column(dst, i):
@@ -364,7 +416,7 @@
 
     def by_row(dst, i):
         for u in range(part_k // 2):
-            s = half + i * part_k + 2 * u
+            s = i * part_k + 2 * u
             o0 = attend(s)
             o1 = attend(s + 1)
             for k in range(4):
@@ -383,46 +435,11 @@
                             dst.dtype
                         )
 
-    def o_partner(i):
-        return dcopy(s0.at[i], r0.at[i], D_O + i, partner)
-
-    def for_partner(i):
-        @pl.when(c == 0)
-        def _():
-            by_row(s0, i)
-
-        @pl.when(c == 1)
-        def _():
-            by_column(s0, i)
-
-        o_partner(i).start()
-
-    loop(2, for_partner)
-
-    ml_partner.wait_recv()
-
-    def mlsend(p):
-        return rcopy(ml1.at[p], rml1.at[a], ML1, p, a, first(p))
-
-    def ml_from(p):
-        return rcopy(ml1.at[p], rml1.at[p], ML1, p, p, first(p))
-
     def osend(i, p):
         return rcopy(s1.at[i, p], r1.at[i, a], O1 + i, p, a, first(p))
 
     def o_from(i, p):
         return rcopy(s1.at[i, p], r1.at[i, p], O1 + i, p, p, first(p))
-
-    for p in range(SIDE):
-        here, there = mlo[c, p], rml0[p]
-        top = jnp.maximum(here, there)
-        f_here = jnp.exp(here - top)
-        f_there = jnp.exp(there - top)
-        total = f_here * pltpu.roll(here, 64, 1) + f_there * pltpu.roll(there, 64, 1)
-        ml1[p] = jnp.where(lane8 < 64, top, pltpu.roll(total, 64, 1))
-        fown[p] = f_here
-        fpar[p] = f_there
-    peers(a, lambda p: mlsend(p).start())
 
     def widen(wide, p, f):
         for k in range(half):
@@ -431,36 +448,16 @@
     def twice(f):
         return jnp.concatenate([f, f], axis=0)
 
-    def widen_both(i):
-        for d in range(2):
-            widen(wown, 2 * i + d, fown[2 * i + d])
-            widen(wpar, 2 * i + d, fpar[2 * i + d])
-
-    loop(SIDE // 2, widen_both)
-
-    def chip_sum(i, p):
-        for k in range(part_k):
-            fh = twice(wown[p, i * part_k + k])
-            ft = twice(wpar[p, i * part_k + k])
-            s1[i, p, k] = (fh * ow[i, p, k] + ft * r0[i, p, k].astype(F32)).astype(BF16)
-
     def for_self(i):
         @pl.when(c == 0)
         def _():
-            by_column(ow, i)
+            by_column(s1, i)
 
         @pl.when(c == 1)
         def _():
-            by_row(ow, i)
-
-        o_partner(i).wait_recv()
-
-        def chip_send(p):
-            chip_sum(i, p)
-            osend(i, p).start()
-
-        peers(a, chip_send)
-        chip_sum(i, a)
+            by_row(s1, i)
+
+        peers(a, lambda p: osend(i, p).start())
 
     loop(2, for_self)
 
@@ -673,18 +670,19 @@
     in_step(1)
     peers(b, lambda p: a2_send(p).start())
     peers(a, lambda p: q1(p).wait_send())
+    loop(SIDE, lambda p: q1_across(p).wait_send())
+    for p in range(parts):
+        k_copy(p).wait_send()
     for d in range(SIDE):
         chunk = at(a, d)
         for slot in (1, 2, 3, 5, 6, 7, 4 if d % 2 == 0 else 0):
             q2(slot, b, chunk, at(b, 1)).wait_send()
-    loop(SIDE, lambda p: qd(p).wait_send())
     peers(a, lambda p: mlsend(p).wait_send())
     for i in range(2):
         peers(a, lambda p: osend(i, p).wait_send())
-        o_partner(i).wait_send()
     peers(b, lambda p: ml2_send(p).wait_send())
     peers(b, lambda p: o2_send(p).wait_send())
-    for copy in to_partner + [ml_partner, swap]:
+    for copy in to_partner + [swap]:
         copy.wait_send()
     peers(b, lambda p: a2_from(p).wait_recv())
     r4[b] = s4[...]
@@ -772,16 +770,12 @@
     scratch = [
         V(queries.shape, BF16),
         V((seqs, 128), F32),
-        V((2, SIDE, SIDE, seqs + 8, 128), BF16),
+        V((seqs, 128), F32),
+        V((ROWS, 128), BF16),
+        V((SIDE, SIDE, 2, ROWS, 128), BF16),
         V((SIDE * A_GROUP, 128), F32),
-        V((H * PITCH, 128), F32),
-        V((seqs, entry, ctx_dev), BF16),
-        V((seqs, H, ctx_dev), BF16),
-        V(chunk, BF16),
-        V(chunk, BF16),
-        V(eights, F32),
-        V(chunk, F32),
-        V((2,) + eights, F32),
+        V((2, half, entry, ctx_dev), BF16),
+        V((half, H, 2 * ctx_dev), BF16),
         V(chunk, BF16),
         V(chunk, BF16),
         V(eights, F32),
@@ -789,8 +783,6 @@
         V((8, 128), F32),
         V(eights, F32),
         V(eights, F32),
-        V(eights, F32),
-        V((SIDE, half, 8, 128), F32),
         V((SIDE, half, 8, 128), F32),
         V((half, 16, 128), F32),
         V((384, 128), F32),
@@ -824,8 +816,10 @@
         pltpu.SemaphoreType.DMA((10, SIDE)),
         pltpu.SemaphoreType.DMA((SIDE, SIDE)),
         pltpu.SemaphoreType.DMA((SIDE, SIDE)),
-        pltpu.SemaphoreType.DMA((10,)),
-        pltpu.SemaphoreType.DMA((10,)),
+        pltpu.SemaphoreType.DMA((half // 2,)),
+        pltpu.SemaphoreType.DMA((half // 2,)),
+        pltpu.SemaphoreType.DMA((7,)),
+        pltpu.SemaphoreType.DMA((7,)),
         pltpu.SemaphoreType.REGULAR((3,)),
     ]
     dispatched, slot_scale, slot_gate = pl.pallas_call(

time: 92.5 us -> 89.1 us (0.963)
  Pallas kernels: 87.7 us -> 84.4 us
    pallas_call x1, Pallas kernels: 87.7 us -> 84.4 us  [per_device(): pl.pallas_call(kernel, out_shape=(jax.ShapeDtypeStruct((experts, CAP, col...]
where the time goes in v4:
time: 89.1 us; the launch traced here: 88.9 us
  Pallas kernels  84.4 us (95%)
  local copies, waits for them, and re-layouts  3.91 us (4%)
    pallas_call x1, Pallas kernels, per_device(): pl.pallas_call(kernel, out_shape=(jax.ShapeDtypeStruct((experts, CAP, col...  84.4 us
    unnamed x3, local copies, waits for them, and re-layouts  3.91 us

profile of v4, /device:TPU:513, one launch (start us, length us, event | category | flops | bytes accessed | tf_op | source)
XLA Modules:
  0.0 88.9 jit_solution(16627211183165944629)
XLA Ops:
  0.6 84.4 %shard_map.112 = (bf16[2,2,7168]{2,1,0:T(2,128)(2,1)}, f32[2,2]{1,0:T(2,128)}, f32[2,2]{1,0:T(2,128)}) custom-call(bf16[40,144]{1,0:T(8,128)(2,1)} %q_in.1, bf16[40,576,128]{2,1,0:T(8,128)(2,1)} %bitcast.4, s32[40]{0:T(128)} %ctx.1, bf16[128,128]{1,0:T(8,128)(2,1)} %vu_in.1, bf16[32,7168]{1,0:T(8,128)(2,1)} %op_in.1, bf16[40,56]{1,0:T(8,128)(2,1)} %res_in.1, ...), custom_call_target="tpu_custom_call" | custom-call | tf_op jit(solution)/shard_map/pallas_call | solution.py:825
  85.0 1.5 %copy.15 = bf16[2,2,7168]{2,1,0:T(2,128)(2,1)} copy(bf16[2,2,7168]{2,1,0:T(2,128)(2,1)} %get-tuple-element.6) | data formatting | bytes 114688
  86.5 1.2 %copy.16 = f32[2,2]{1,0:T(2,128)} copy(f32[2,2]{1,0:T(2,128)} %get-tuple-element.7) | data formatting | bytes 32
  87.7 1.2 %copy.17 = f32[2,2]{1,0:T(2,128)} copy(f32[2,2]{1,0:T(2,128)} %get-tuple-element.8) | data formatting | bytes 32

commit v5 on v4

--- a/solution.py
+++ b/solution.py
@@ -21,6 +21,10 @@
 A_GROUP = QUARTERS * PITCH + 8
 KV = ("kv_0", "kv_1", "kv_2")
 GROUPS_KV = ("groups", "kv_0", "kv_1", "kv_2")
+FAR_FIRST = (4, 3, 5, 2, 6, 1, 7)
+DIRECT = (3, 4, 5)
+PARTS = 2
+CUTS = (0, 4, 7)
 MESH = pl.DeviceIdType.MESH
 F32 = jnp.float32
 BF16 = jnp.bfloat16
@@ -29,8 +33,9 @@
 masked_score = -1e30
 small_eps = 1e-06
 
-Q1, Q1B, O1, O1B, ML1, ML2, O2, A1, A2, A3 = range(10)
-D_VU, D_RES, D_GAIN, D_W, D_F, D_X, D_V = range(7)
+Q1, Q1B, ML1, ML2, O2, A1, A2, A3, O1 = 0, 1, 2, 3, 4, 5, 7, 9, 11
+PHASES = O1 + PARTS
+D_VU, D_RES, D_GAIN, D_W, D_F, D_X, D_N, D_NW = range(8)
 
 
 def lanes(shape):
@@ -49,17 +54,21 @@
     lax.fori_loop(0, count, step, 0)
 
 
+def padded(tiles, half):
+    return -(-tiles * (half + 1) // 8) * 8
+
+
 def far_first(i):
     return SIDE // 2 + (1 - 2 * lax.rem(i, 2)) * lax.div(i + 1, 2)
 
 
 def kernel(
-    q_in, cache_in, ctx, vu_in, op_in, res_in, gain_in, ids_in, gate_in,
+    q_in, cache_in, ctx_in, vu_in, op_in, res_in, gain_in, ids_in, gate_in,
     disp_out, scale_out, gate_out,
     qraw, ext, main, qs, qb, qa, cache, wb, s1, r1, ml1, rml1,
-    ml2, rml2, fown, wown, acc, ab, s2, r2, vu, vs, vr, res, gain, ta, tb, lhs, w,
+    ml2, rml2, fown, wown, acc, ab, s2, r2, vu, res, gain, ta, tb, lhs, w,
     s3, r3, s4, r4, rf, ids, gate, pt, pick, y, fs, fr, xs, xr,
-    loc, ssem, rsem, qsend, qrecv, ksend, krecv, dsend, drecv, steps,
+    ctx, loc, ssem, rsem, qsend, qrecv, ksend, krecv, dsend, drecv, steps,
 ):
     g = lax.axis_index("groups")
     yy = lax.axis_index("kv_0")
@@ -102,6 +111,10 @@
         )
 
     def peers(me, body):
+        for d in FAR_FIRST:
+            body(lax.rem(me + d, SIDE))
+
+    def peers_loop(me, body):
         def one(i):
             body(lax.rem(me + far_first(i), SIDE))
 
@@ -118,6 +131,7 @@
         local(res_in, res.at[c], 2),
         local(gain_in, gain.at[c], 23),
         local(ids_in, ids, 3),
+        local(ctx_in, ctx, 24),
         local(gate_in, gate, 4),
     ]
     for copy in small:
@@ -217,7 +231,7 @@
             if d:
                 q1_from(chunk, c).wait_recv()
             q1_from(chunk, 1 - c).wait_recv()
-            for e in (2, 6, 1, 7):
+            for e in FAR_FIRST if d in DIRECT else (2, 6, 1, 7):
                 q2(e, b, chunk, at(b, e)).start()
 
     def relay(distances):
@@ -233,6 +247,19 @@
             q2(5, source, chunk, at(b, 7)).start()
             if d % 2 == 1:
                 q2(0, source, chunk, at(b, 6)).start()
+
+    for copy in w_loads:
+        copy.wait()
+    w_rows = w.at[:, pl.ds(w_row, 32), :]
+    beside = pl.multiple_of((1 - half_x) * 64 + c * 32, 32)
+    w_beside = w.at[:, pl.ds(beside, 32), :]
+    w_out = dcopy(w_rows, w_rows, D_N, neighbour)
+    w_in = dcopy(w_beside, w_beside, D_N, neighbour)
+    w_across = dcopy(w_beside, w_beside, D_NW, partner)
+
+    @pl.when(c == 0)
+    def _():
+        w_out.start()
 
     spread((0,))
     k_copy(0).start()
@@ -250,16 +277,16 @@
     k_copy(6).start()
     relay((2, 6))
     k_copy(7).start()
-    relay((3, 5))
+    relay([d for d in (3, 5, 4) if d not in DIRECT])
     k_copy(8).start()
-    relay((4,))
     k_copy(9).start()
+
+    @pl.when(c == 1)
+    def _():
+        w_out.start()
 
     for copy in small:
         copy.wait()
-    for copy in w_loads:
-        copy.wait()
-    w_rows = w.at[:, pl.ds(w_row, 32), :]
     to_partner = [
         dcopy(vu.at[c], vu.at[c], D_VU, partner),
         dcopy(res.at[c], res.at[c], D_RES, partner),
@@ -271,9 +298,12 @@
 
     for ref in (ml1, ab, ta, tb, pt):
         ref[...] = jnp.zeros(ref.shape, F32)
-    for e in (1, 7, 3, 5, 4):
-        source = at(b, e)
-        loop(SIDE, lambda k: q2(1, source, k, source).wait_recv())
+    for d in range(SIDE):
+        chunk = at(a, d)
+        for e in range(1, SIDE):
+            if d in DIRECT or e not in (2, 6):
+                source = at(b, e)
+                q2(1, source, chunk, source).wait_recv()
     to_partner[3].start()
 
     lane = lanes((ROWS, 128))
@@ -320,7 +350,8 @@
     for p in range(parts):
         k_from(p).wait_recv()
     position = chip * 2 * ctx_dev + lanes((1, 2 * ctx_dev))
-    part_k = half // 2
+    part_k = half // PARTS
+    many = half // 2
 
     def weigh(s, by_column):
         pieces = []
@@ -354,8 +385,8 @@
 
     def weigh_columns(i):
         tiles_m = [jnp.zeros((8, 128), F32) for _ in range(4)]
-        for u in range(part_k):
-            s = i * part_k + u
+        for u in range(many):
+            s = i * many + u
             top, total = weigh(s, True)
             for k in range(4):
                 rows = slice(8 * k, 8 * k + 8)
@@ -366,8 +397,8 @@
 
     def weigh_rows(i):
         tiles_m = [jnp.zeros((8, 128), F32) for _ in range(SIDE)]
-        for u in range(part_k // 2):
-            pair = i * (part_k // 2) + u
+        for u in range(many // 2):
+            pair = i * (many // 2) + u
             t0, l0 = weigh(2 * pair, False)
             t1, l1 = weigh(2 * pair + 1, False)
             for k in range(4):
@@ -459,7 +490,7 @@
 
         peers(a, lambda p: osend(i, p).start())
 
-    loop(2, for_self)
+    loop(PARTS, for_self)
 
     peers(a, lambda p: ml_from(p).wait_recv())
     rml1[a] = ml1[a]
@@ -488,11 +519,8 @@
 
     loop(SIDE // 2, widen_row)
 
-    idle_row = pl.multiple_of((1 - half_x) * 64, 64)
 
     def fill(p):
-        w[p, pl.ds(idle_row, 64), :] = jnp.zeros((64, width), BF16)
-
         def block(k):
             start = pl.multiple_of(k * 16, 16)
             row = start + sublanes((16, width))
@@ -535,6 +563,9 @@
     own = jnp.where(c == 0, pt[...], pltpu.roll(pt[...], 128 - half, 1))
     pick[...] = jnp.where(lanes((16, 128)) < half, own, 0.0)
 
+    w_in.wait_recv()
+    w_across.start()
+
     for copy in to_partner[:3]:
         copy.wait_recv()
     ta[0:seqs, 0:56] = res[0].astype(F32)
@@ -561,9 +592,9 @@
             o_from(i, p).wait_recv()
             add(r1.at[i, p], i, p, False)
 
-        peers(a, take)
-
-    loop(2, gather)
+        peers_loop(a, take)
+
+    loop(PARTS, gather)
     peers(b, lambda p: ml2_from(p).wait_recv())
     rml2[b] = packed
     top = rml2[0]
@@ -618,92 +649,112 @@
         low = (block - high.astype(F32)).astype(BF16)
         part = part + jnp.dot(high, vu[k], preferred_element_type=F32)
         part = part + jnp.dot(low, vu[k], preferred_element_type=F32)
-    vs[...] = part
-    swap = dcopy(vs, vr, D_V, neighbour)
-    swap.start()
     to_partner[3].wait_recv()
-    swap.wait_recv()
-    left = jnp.concatenate([(part + vr[...]).astype(BF16), lhs[...].astype(BF16)], axis=1)
-
-    def a1_send(p):
-        return rcopy(s3.at[p], r3.at[a], A1, p, a, first(p))
-
-    def a1_from(p):
-        return rcopy(s3.at[p], r3.at[p], A1, p, p, first(p))
-
-    def a2_send(p):
-        return rcopy(s4, r4.at[b], A2, p, b, second(p))
-
-    def a2_from(p):
-        return rcopy(s4, r4.at[p], A2, p, p, second(p))
-
-    def a3_send(p):
-        return rcopy(rf.at[a], rf.at[a], A3, p, a, first(p))
-
-    def a3_from(p):
-        return rcopy(rf.at[p], rf.at[p], A3, p, p, first(p))
+    w_across.wait_recv()
+    left = jnp.concatenate([part.astype(BF16), lhs[...].astype(BF16)], axis=1)
+
+    def part_rows(j):
+        sizes = [padded(CUTS[k + 1] - CUTS[k], half) for k in range(2)]
+        return pl.ds(sum(sizes[:j]), sizes[j])
+
+    def a1_send(j, p):
+        rows = part_rows(j)
+        return rcopy(s3.at[p, rows], r3.at[a, rows], A1 + j, p, a, first(p))
+
+    def a1_from(j, p):
+        rows = part_rows(j)
+        return rcopy(s3.at[p, rows], r3.at[p, rows], A1 + j, p, p, first(p))
+
+    def a2_send(j, p):
+        rows = part_rows(j)
+        return rcopy(s4.at[rows], r4.at[b, rows], A2 + j, p, b, second(p))
+
+    def a2_from(j, p):
+        rows = part_rows(j)
+        return rcopy(s4.at[rows], r4.at[p, rows], A2 + j, p, p, second(p))
+
+    def a3_send(j, p):
+        rows = part_rows(j)
+        return rcopy(rf.at[a, rows], rf.at[a, rows], A3 + j, p, a, first(p))
+
+    def a3_from(j, p):
+        rows = part_rows(j)
+        return rcopy(rf.at[p, rows], rf.at[p, rows], A3 + j, p, p, first(p))
 
     def in_step(k):
         pl.semaphore_signal(steps.at[k], inc=1, device_id=partner, device_id_type=MESH)
         pl.semaphore_wait(steps.at[k], 1)
 
-    def project(p):
-        out = jnp.dot(left, w[p], preferred_element_type=F32)
-        blocks = [out[:half, 128 * t : 128 * t + 128] for t in range(tiles)]
-        blocks += [out[half : half + 1, 128 * t : 128 * t + 128] for t in range(tiles)]
-        blocks.append(jnp.zeros((rf.shape[1] - tiles * (half + 1), 128), F32))
-        s3[p] = jnp.concatenate(blocks, axis=0).astype(BF16)
-
-    def project_send(p):
-        project(p)
-        a1_send(p).start()
+    def project(j, p):
+        out = jnp.dot(left, w[p, :, 128 * CUTS[j] : 128 * CUTS[j + 1]], preferred_element_type=F32)
+        count = CUTS[j + 1] - CUTS[j]
+        blocks = [out[:half, 128 * t : 128 * t + 128] for t in range(count)]
+        blocks += [out[half : half + 1, 128 * t : 128 * t + 128] for t in range(count)]
+        blocks.append(jnp.zeros((padded(count, half) - count * (half + 1), 128), F32))
+        s3[p, part_rows(j), :] = jnp.concatenate(blocks, axis=0).astype(BF16)
+
+    def total_of(ref, j):
+        total = ref[0, part_rows(j), :].astype(F32)
+        for p in range(1, SIDE):
+            total = total + ref[p, part_rows(j), :].astype(F32)
+        return total.astype(BF16)
 
     in_step(0)
-    peers(a, project_send)
-    project(a)
-    peers(a, lambda p: a1_from(p).wait_recv())
-    r3[a] = s3[a]
-    total = r3[0].astype(F32)
-    for p in range(1, SIDE):
-        total = total + r3[p].astype(F32)
-    s4[...] = total.astype(BF16)
-    in_step(1)
-    peers(b, lambda p: a2_send(p).start())
+    for j in range(2):
+
+        def project_send(p):
+            project(j, p)
+            a1_send(j, p).start()
+
+        peers_loop(a, project_send)
+        project(j, a)
+    for j in range(2):
+        peers(a, lambda p: a1_from(j, p).wait_recv())
+        r3[a, part_rows(j), :] = s3[a, part_rows(j), :]
+        s4[part_rows(j), :] = total_of(r3, j)
+        if j == 0:
+            in_step(1)
+        peers(b, lambda p: a2_send(j, p).start())
     peers(a, lambda p: q1(p).wait_send())
     loop(SIDE, lambda p: q1_across(p).wait_send())
     for p in range(parts):
         k_copy(p).wait_send()
     for d in range(SIDE):
         chunk = at(a, d)
-        for slot in (1, 2, 3, 5, 6, 7, 4 if d % 2 == 0 else 0):
+        for slot in range(1, SIDE) if d in DIRECT else (1, 2, 3, 5, 6, 7, 4 if d % 2 == 0 else 0):
             q2(slot, b, chunk, at(b, 1)).wait_send()
     peers(a, lambda p: mlsend(p).wait_send())
-    for i in range(2):
+    for i in range(PARTS):
         peers(a, lambda p: osend(i, p).wait_send())
     peers(b, lambda p: ml2_send(p).wait_send())
     peers(b, lambda p: o2_send(p).wait_send())
-    for copy in to_partner + [swap]:
+    for copy in to_partner + [w_out, w_across]:
         copy.wait_send()
-    peers(b, lambda p: a2_from(p).wait_recv())
-    r4[b] = s4[...]
-    total = r4[0].astype(F32)
-    for p in range(1, SIDE):
-        total = total + r4[p].astype(F32)
-    rf[a] = total.astype(BF16)
-    in_step(2)
-    peers(a, lambda p: a3_send(p).start())
-    peers(a, lambda p: a1_send(p).wait_send())
-    peers(b, lambda p: a2_send(p).wait_send())
-    peers(a, lambda p: a3_from(p).wait_recv())
+    for j in range(2):
+        peers(b, lambda p: a2_from(j, p).wait_recv())
+        r4[b, part_rows(j), :] = s4[part_rows(j), :]
+        rf[a, part_rows(j), :] = total_of(r4, j)
+        if j == 0:
+            in_step(2)
+        peers(a, lambda p: a3_send(j, p).start())
+    for j in range(2):
+        peers(a, lambda p: a1_send(j, p).wait_send())
+        peers(b, lambda p: a2_send(j, p).wait_send())
+    for j in range(2):
+        peers(a, lambda p: a3_from(j, p).wait_recv())
 
     choose = pick[...][:, 0:half]
     choose_b = choose.astype(BF16)
     squares = jnp.zeros((half, 128), F32)
     largest = jnp.zeros((half, 128), F32)
     for p in range(SIDE):
-        block = rf[p].astype(F32)
-        parts_r = [block[half * t : half * (t + 1)] for t in range(tiles)]
-        gains = [block[half * tiles + t : half * tiles + t + 1] for t in range(tiles)]
+        parts_r = []
+        gains = []
+        for j in range(2):
+            block = rf[p, part_rows(j), :].astype(F32)
+            count = CUTS[j + 1] - CUTS[j]
+            parts_r += [block[half * t : half * (t + 1)] for t in range(count)]
+            gains += [block[half * count + t : half * count + t + 1] for t in range(count)]
         for v, gv in zip(parts_r, gains):
             squares = squares + v * v
             largest = jnp.maximum(largest, jnp.abs(v * gv))
@@ -745,7 +796,8 @@
             for e in range(2):
                 disp_out[e, :, pl.ds(p * width, width)] = rows[CAP * e : CAP * e + CAP]
 
-    peers(a, lambda p: a3_send(p).wait_send())
+    for j in range(2):
+        peers(a, lambda p: a3_send(j, p).wait_send())
     x_partner.wait_send()
     f_partner.wait_send()
 
@@ -760,12 +812,11 @@
     width = columns // SIDE
     piece = residual.shape[1]
     experts = 2
-    rows = -(-(width // 128) * (half + 1) // 8) * 8
+    rows = sum(padded(CUTS[k + 1] - CUTS[k], half) for k in range(2))
     any_space = pl.BlockSpec(memory_space=pl.ANY)
     vmem = pl.BlockSpec(memory_space=pltpu.VMEM)
-    smem = pl.BlockSpec(memory_space=pltpu.SMEM)
     V = pltpu.VMEM
-    chunk = (2, SIDE, half // 2, 16, 128)
+    chunk = (PARTS, SIDE, half // PARTS, 16, 128)
     eights = (SIDE, 8, 128)
     scratch = [
         V(queries.shape, BF16),
@@ -789,8 +840,6 @@
         V((SIDE, 2 * ROWS, 128), BF16),
         V((SIDE, 2 * ROWS, 128), BF16),
         V((2, 128, VD), BF16),
-        V((ROWS, VD), F32),
-        V((ROWS, VD), F32),
         V((2, seqs, piece), BF16),
         V((2, 1, piece), BF16),
         V((seqs + 8, 128), F32),
@@ -811,15 +860,16 @@
         V((SIDE // 2, 16, width), BF16),
         V((8, 128), F32),
         V((8, 128), F32),
-        pltpu.SemaphoreType.DMA((24,)),
-        pltpu.SemaphoreType.DMA((10, SIDE)),
-        pltpu.SemaphoreType.DMA((10, SIDE)),
+        pltpu.SMEM(context_lengths.shape, jnp.int32),
+        pltpu.SemaphoreType.DMA((25,)),
+        pltpu.SemaphoreType.DMA((PHASES, SIDE)),
+        pltpu.SemaphoreType.DMA((PHASES, SIDE)),
         pltpu.SemaphoreType.DMA((SIDE, SIDE)),
         pltpu.SemaphoreType.DMA((SIDE, SIDE)),
         pltpu.SemaphoreType.DMA((half // 2,)),
         pltpu.SemaphoreType.DMA((half // 2,)),
-        pltpu.SemaphoreType.DMA((7,)),
-        pltpu.SemaphoreType.DMA((7,)),
+        pltpu.SemaphoreType.DMA((8,)),
+        pltpu.SemaphoreType.DMA((8,)),
         pltpu.SemaphoreType.REGULAR((3,)),
     ]
     dispatched, slot_scale, slot_gate = pl.pallas_call(
@@ -829,7 +879,7 @@
             jax.ShapeDtypeStruct((experts, CAP), F32),
             jax.ShapeDtypeStruct((experts, CAP), F32),
         ),
-        in_specs=[any_space, any_space, smem] + [any_space] * 6,
+        in_specs=[any_space] * 9,
         out_specs=(vmem, vmem, vmem),
         scratch_shapes=scratch,
         compiler_params=pltpu.CompilerParams(collective_id=0, has_side_effects=True),
@@ -837,7 +887,17 @@
         queries, latent_cache.transpose(0, 2, 1), context_lengths, value_up, out_proj, residual,
         norm_gain[None, :], expert_ids.T, gate_weights.T,
     )
-    return dispatched, slot_scale, slot_gate
+    def hand_over(*refs):
+        for source, target in zip(refs[:3], refs[3:]):
+            target[...] = source[...]
+
+    results = (dispatched, slot_scale, slot_gate)
+    return pl.pallas_call(
+        hand_over,
+        out_shape=tuple(jax.ShapeDtypeStruct(r.shape, r.dtype) for r in results),
+        in_specs=[vmem] * 3,
+        out_specs=(vmem,) * 3,
+    )(*results)
 
 
 def solution(mesh):

time: 89.1 us -> 81.2 us (0.911)
  Pallas kernels: 84.4 us -> 80.4 us
  local copies, waits for them, and re-layouts: 3.91 us -> 0 us
    pallas_call x1, Pallas kernels: 84.4 us -> 78.9 us  [per_device(): pl.pallas_call(kernel, out_shape=(jax.ShapeDtypeStruct((experts, CAP, col...]
    unnamed x3 -> x0, local copies, waits for them, and re-layouts: 3.91 us -> none
    pallas_call x0 -> x1, Pallas kernels: none -> 1.46 us  [per_device(): pl.pallas_call(hand_over, out_shape=tuple((jax.ShapeDtypeStruct(r.shape,...]
where the time goes in v5:
time: 81.2 us; the launch traced here: 81 us
  Pallas kernels  80.4 us (99%)
    pallas_call x1, Pallas kernels, per_device(): pl.pallas_call(kernel, out_shape=(jax.ShapeDtypeStruct((experts, CAP, col...  78.9 us

profile of v5, /device:TPU:513, one launch (start us, length us, event | category | flops | bytes accessed | tf_op | source)
XLA Modules:
  0.0 81.0 jit_solution(9724696676300808021)
XLA Ops:
  0.6 78.9 %shard_map.112 = (bf16[2,2,7168]{2,1,0:T(2,128)(2,1)}, f32[2,2]{1,0:T(2,128)}, f32[2,2]{1,0:T(2,128)}) custom-call(bf16[40,144]{1,0:T(8,128)(2,1)} %q_in.1, bf16[40,576,128]{2,1,0:T(8,128)(2,1)} %bitcast.4, s32[40]{0:T(128)} %ctx_in.1, bf16[128,128]{1,0:T(8,128)(2,1)} %vu_in.1, bf16[32,7168]{1,0:T(8,128)(2,1)} %op_in.1, bf16[40,56]{1,0:T(8,128)(2,1)} %res_in.1, ...), custom_call_target="tpu_custom_call" | custom-call | tf_op jit(solution)/shard_map/pallas_call | solution.py:875
  79.6 1.5 %shard_map.113 = (bf16[2,2,7168]{2,1,0:T(2,128)(2,1)}, f32[2,2]{1,0:T(2,128)}, f32[2,2]{1,0:T(2,128)}) custom-call(bf16[2,2,7168]{2,1,0:T(2,128)(2,1)} %get-tuple-element.6.refs_0_, f32[2,2]{1,0:T(2,128)} %get-tuple-element.7.refs_1_, f32[2,2]{1,0:T(2,128)} %get-tuple-element.8.refs_2_), custom_call_target="tpu_custom_call" | custom-call | tf_op jit(solution)/shard_map/pallas_call | solution.py:895

commit v6 on v5

--- a/solution.py
+++ b/solution.py
@@ -33,9 +33,10 @@
 masked_score = -1e30
 small_eps = 1e-06
 
-Q1, Q1B, ML1, ML2, O2, A1, A2, A3, O1 = 0, 1, 2, 3, 4, 5, 7, 9, 11
-PHASES = O1 + PARTS
-D_VU, D_RES, D_GAIN, D_W, D_F, D_X, D_N, D_NW = range(8)
+Q1, Q1B, ML2, O2, A1, A2, A3, O1 = 0, 1, 2, 3, 4, 6, 8, 10
+ML1 = O1 + PARTS
+PHASES = ML1 + PARTS
+D_VU, D_RES, D_GAIN, D_W, D_F, D_X, D_NW, D_N = range(8)
 
 
 def lanes(shape):
@@ -235,7 +236,7 @@
                 q2(e, b, chunk, at(b, e)).start()
 
     def relay(distances):
-        for d in distances:
+        for d in [d for d in distances if d not in DIRECT]:
             chunk = at(a, d)
             source = at(b, 6)
             q2(1, source, chunk, source).wait_recv()
@@ -253,13 +254,18 @@
     w_rows = w.at[:, pl.ds(w_row, 32), :]
     beside = pl.multiple_of((1 - half_x) * 64 + c * 32, 32)
     w_beside = w.at[:, pl.ds(beside, 32), :]
-    w_out = dcopy(w_rows, w_rows, D_N, neighbour)
-    w_in = dcopy(w_beside, w_beside, D_N, neighbour)
+    w_out, w_in = [], []
+    for k in range(2):
+        some = pl.ds(k * (SIDE // 2), SIDE // 2)
+        ours, theirs = w.at[some, pl.ds(w_row, 32), :], w.at[some, pl.ds(beside, 32), :]
+        w_out.append(dcopy(ours, ours, D_N + k, neighbour))
+        w_in.append(dcopy(theirs, theirs, D_N + k, neighbour))
     w_across = dcopy(w_beside, w_beside, D_NW, partner)
 
     @pl.when(c == 0)
     def _():
-        w_out.start()
+        w_out[0].start()
+        w_out[1].start()
 
     spread((0,))
     k_copy(0).start()
@@ -277,13 +283,11 @@
     k_copy(6).start()
     relay((2, 6))
     k_copy(7).start()
-    relay([d for d in (3, 5, 4) if d not in DIRECT])
+    relay((3, 5, 4))
+    pl.when(c == 1)(w_out[0].start)
     k_copy(8).start()
     k_copy(9).start()
 
-    @pl.when(c == 1)
-    def _():
-        w_out.start()
 
     for copy in small:
         copy.wait()
@@ -296,14 +300,8 @@
     for copy in to_partner[:3]:
         copy.start()
 
-    for ref in (ml1, ab, ta, tb, pt):
+    for ref in (ab, ta, tb, pt):
         ref[...] = jnp.zeros(ref.shape, F32)
-    for d in range(SIDE):
-        chunk = at(a, d)
-        for e in range(1, SIDE):
-            if d in DIRECT or e not in (2, 6):
-                source = at(b, e)
-                q2(1, source, chunk, source).wait_recv()
     to_partner[3].start()
 
     lane = lanes((ROWS, 128))
@@ -343,7 +341,25 @@
             for t in range(5):
                 qa[pl.ds(pl.multiple_of(base + t * ROWS, 8), ROWS), :] = whole[t]
 
-    loop(SIDE, assemble)
+    def missing(d, e):
+        if e and (d in DIRECT or e not in (2, 6)):
+            chunk, source = at(a, d), at(b, e)
+            q2(1, source, chunk, source).wait_recv()
+
+    @pl.when(c == 0)
+    def _():
+        for e in (0, 2, 6, 1, 7, 3, 5, 4):
+            for d in (0, 1, 7, 2, 6, 3, 5, 4):
+                missing(d, e)
+            assemble(at(b, e))
+
+    @pl.when(c == 1)
+    def _():
+        for d in (0, 1, 7, 2, 6, 3, 5, 4):
+            for e in (2, 6, 1, 7, 3, 5, 4):
+                missing(d, e)
+            assemble(at(a, d))
+
 
     for copy in k_loads:
         copy.wait()
@@ -351,7 +367,7 @@
         k_from(p).wait_recv()
     position = chip * 2 * ctx_dev + lanes((1, 2 * ctx_dev))
     part_k = half // PARTS
-    many = half // 2
+    many = half // PARTS
 
     def weigh(s, by_column):
         pieces = []
@@ -393,7 +409,7 @@
                 tiles_m[k] = put(tiles_m[k], s, top[rows], total[rows])
         for k in range(4):
             for d in range(2):
-                ml1[2 * k + d] += tiles_m[k]
+                ml1[i, 2 * k + d] = tiles_m[k]
 
     def weigh_rows(i):
         tiles_m = [jnp.zeros((8, 128), F32) for _ in range(SIDE)]
@@ -411,23 +427,13 @@
                         tile = tiles_m[2 * k + d]
                         tiles_m[2 * k + d] = put(tile, 2 * pair + e, top, total)
         for p in range(SIDE):
-            ml1[p] += tiles_m[p]
-
-    @pl.when(c == 0)
-    def _():
-        loop(2, weigh_columns)
-
-    @pl.when(c == 1)
-    def _():
-        loop(2, weigh_rows)
-
-    def mlsend(p):
-        return rcopy(ml1.at[p], rml1.at[a], ML1, p, a, first(p))
-
-    def ml_from(p):
-        return rcopy(ml1.at[p], rml1.at[p], ML1, p, p, first(p))
-
-    peers(a, lambda p: mlsend(p).start())
+            ml1[i, p] = tiles_m[p]
+
+    def mlsend(i, p):
+        return rcopy(ml1.at[i, p], rml1.at[i, a], ML1 + i, p, a, first(p))
+
+    def ml_from(i, p):
+        return rcopy(ml1.at[i, p], rml1.at[i, p], ML1 + i, p, p, first(p))
 
     def attend(s):
         values = jnp.concatenate([cache[0, s, 0:LAT, :], cache[1, s, 0:LAT, :]], axis=1)
@@ -472,52 +478,18 @@
     def o_from(i, p):
         return rcopy(s1.at[i, p], r1.at[i, p], O1 + i, p, p, first(p))
 
-    def widen(wide, p, f):
-        for k in range(half):
-            wide[p, k] = jnp.broadcast_to(f[:, k : k + 1], (8, 128))
-
     def twice(f):
         return jnp.concatenate([f, f], axis=0)
 
-    def for_self(i):
-        @pl.when(c == 0)
-        def _():
-            by_column(s1, i)
-
-        @pl.when(c == 1)
-        def _():
-            by_row(s1, i)
-
+    def on_core(columns, rows):
+        pl.when(c == 0)(columns)
+        pl.when(c == 1)(rows)
+
+    for i in range(PARTS):
+        on_core(lambda: weigh_columns(i), lambda: weigh_rows(i))
+        peers(a, lambda p: mlsend(i, p).start())
+        on_core(lambda: by_column(s1, i), lambda: by_row(s1, i))
         peers(a, lambda p: osend(i, p).start())
-
-    loop(PARTS, for_self)
-
-    peers(a, lambda p: ml_from(p).wait_recv())
-    rml1[a] = ml1[a]
-    row_top = rml1[0]
-    for p in range(1, SIDE):
-        row_top = jnp.maximum(row_top, rml1[p])
-    total = jnp.zeros((8, 128), F32)
-    for p in range(SIDE):
-        factor = jnp.exp(rml1[p] - row_top)
-        total = total + factor * pltpu.roll(rml1[p], 64, 1)
-        fown[p] = factor
-    packed = jnp.where(lane8 < 64, row_top, pltpu.roll(total, 64, 1))
-    ml2[...] = packed
-
-    def ml2_send(p):
-        return rcopy(ml2, rml2.at[b], ML2, p, b, second(p))
-
-    def ml2_from(p):
-        return rcopy(ml2, rml2.at[p], ML2, p, p, second(p))
-
-    peers(b, lambda p: ml2_send(p).start())
-
-    def widen_row(i):
-        for d in range(2):
-            widen(wown, 2 * i + d, fown[2 * i + d])
-
-    loop(SIDE // 2, widen_row)
 
 
     def fill(p):
@@ -563,9 +535,6 @@
     own = jnp.where(c == 0, pt[...], pltpu.roll(pt[...], 128 - half, 1))
     pick[...] = jnp.where(lanes((16, 128)) < half, own, 0.0)
 
-    w_in.wait_recv()
-    w_across.start()
-
     for copy in to_partner[:3]:
         copy.wait_recv()
     ta[0:seqs, 0:56] = res[0].astype(F32)
@@ -579,13 +548,42 @@
     gain_row = jnp.broadcast_to(ta[seqs : seqs + 1, :], (ROWS, 128))
     lhs[...] = jnp.where(row < half, mine, jnp.where(row == half, gain_row, 0.0))
 
+    def ml2_send(p):
+        return rcopy(ml2, rml2.at[b], ML2, p, b, second(p))
+
+    def ml2_from(p):
+        return rcopy(ml2, rml2.at[p], ML2, p, p, second(p))
+
     def add(block, i, p, fresh):
         for k in range(part_k):
+            term = twice(wown[p, k]) * block[k].astype(F32)
             index = i * part_k + k
-            term = twice(wown[p, index]) * block[k].astype(F32)
             acc[index] = term if fresh else acc[index] + term
 
-    def gather(i):
+    packed = jnp.zeros((8, 128), F32)
+    for i in range(PARTS):
+        peers(a, lambda p: ml_from(i, p).wait_recv())
+        rml1[i, a] = ml1[i, a]
+        row_top = rml1[i, 0]
+        for p in range(1, SIDE):
+            row_top = jnp.maximum(row_top, rml1[i, p])
+        total = jnp.zeros((8, 128), F32)
+        for p in range(SIDE):
+            factor = jnp.exp(rml1[i, p] - row_top)
+            total = total + factor * pltpu.roll(rml1[i, p], 64, 1)
+            fown[p] = factor
+        both = jnp.where(lane8 < 64, row_top, pltpu.roll(total, 64, 1))
+        group = lax.rem(lane8, 64)
+        packed = jnp.where((group >= i * part_k) & (group < (i + 1) * part_k), both, packed)
+        if i == PARTS - 1:
+            ml2[...] = packed
+            peers(b, lambda p: ml2_send(p).start())
+            pl.when(c == 1)(w_out[1].start)
+        for p in range(SIDE):
+            f = fown[p]
+            for k in range(part_k):
+                lane_k = i * part_k + k
+                wown[p, k] = jnp.broadcast_to(f[:, lane_k : lane_k + 1], (8, 128))
         add(s1.at[i, a], i, a, True)
 
         def take(p):
@@ -593,19 +591,6 @@
             add(r1.at[i, p], i, p, False)
 
         peers_loop(a, take)
-
-    loop(PARTS, gather)
-    peers(b, lambda p: ml2_from(p).wait_recv())
-    rml2[b] = packed
-    top = rml2[0]
-    for p in range(1, SIDE):
-        top = jnp.maximum(top, rml2[p])
-    total = jnp.zeros((8, 128), F32)
-    for p in range(SIDE):
-        total = total + jnp.exp(rml2[p] - top) * pltpu.roll(rml2[p], 64, 1)
-    final = jnp.exp(row_top - top) / total
-    for k in range(half):
-        acc[k] = acc[k] * twice(jnp.broadcast_to(final[:, k : k + 1], (8, 128)))
 
     @pl.when(c == 0)
     def _():
@@ -636,11 +621,31 @@
         return rcopy(s2.at[p], r2.at[p], O2, p, p, second(p))
 
     peers(b, lambda p: o2_send(p).start())
+    peers(b, lambda p: ml2_from(p).wait_recv())
+    rml2[b] = packed
+    row_even = b - c * (b - lax.div(b, 2))
+    row_odd = row_even + 4 * c
+    even = lax.rem(lanes((1, 128)), 2) == 0
+    each_ml = jnp.concatenate(
+        [
+            jnp.where(even, rml2[p, pl.ds(row_even, 1), :], rml2[p, pl.ds(row_odd, 1), :])
+            for p in range(SIDE)
+        ],
+        axis=0,
+    )
+    factor = jnp.exp(each_ml - jnp.max(each_ml, axis=0, keepdims=True))
+    total = jnp.sum(factor * pltpu.roll(each_ml, 64, 1), axis=0, keepdims=True)
+    factor = jnp.where(lane8 < half, factor / total, 0.0)
+    factor = jnp.concatenate([factor, jnp.zeros((120, 128), F32)], axis=0).T
+    factors = [jnp.broadcast_to(factor[0:ROWS, p : p + 1], (ROWS, 128)) for p in range(SIDE)]
+    for copy in w_in:
+        copy.wait_recv()
+    w_across.start()
     peers(b, lambda p: o2_from(p).wait_recv())
     r2[b] = s2[b]
-    merged = r2[0].astype(F32)
+    merged = twice(factors[0]) * r2[0].astype(F32)
     for p in range(1, SIDE):
-        merged = merged + r2[p].astype(F32)
+        merged = merged + twice(factors[p]) * r2[p].astype(F32)
 
     part = jnp.zeros((ROWS, VD), F32)
     for k in range(2):
@@ -702,11 +707,12 @@
     in_step(0)
     for j in range(2):
 
-        def project_send(p):
-            project(j, p)
-            a1_send(j, p).start()
-
-        peers_loop(a, project_send)
+        for batch in ((4, 3, 5), (2, 6, 1, 7)):
+            for d in batch:
+                project(j, at(a, d))
+            for d in batch:
+                a1_send(j, at(a, d)).start()
+    for j in range(2):
         project(j, a)
     for j in range(2):
         peers(a, lambda p: a1_from(j, p).wait_recv())
@@ -723,12 +729,13 @@
         chunk = at(a, d)
         for slot in range(1, SIDE) if d in DIRECT else (1, 2, 3, 5, 6, 7, 4 if d % 2 == 0 else 0):
             q2(slot, b, chunk, at(b, 1)).wait_send()
-    peers(a, lambda p: mlsend(p).wait_send())
+    for i in range(PARTS):
+        peers(a, lambda p: mlsend(i, p).wait_send())
     for i in range(PARTS):
         peers(a, lambda p: osend(i, p).wait_send())
     peers(b, lambda p: ml2_send(p).wait_send())
     peers(b, lambda p: o2_send(p).wait_send())
-    for copy in to_partner + [w_out, w_across]:
+    for copy in to_partner + w_out + [w_across]:
         copy.wait_send()
     for j in range(2):
         peers(b, lambda p: a2_from(j, p).wait_recv())
@@ -829,12 +836,12 @@
         V((half, H, 2 * ctx_dev), BF16),
         V(chunk, BF16),
         V(chunk, BF16),
-        V(eights, F32),
-        V(eights, F32),
+        V((PARTS,) + eights, F32),
+        V((PARTS,) + eights, F32),
         V((8, 128), F32),
         V(eights, F32),
         V(eights, F32),
-        V((SIDE, half, 8, 128), F32),
+        V((SIDE, half // PARTS, 8, 128), F32),
         V((half, 16, 128), F32),
         V((384, 128), F32),
         V((SIDE, 2 * ROWS, 128), BF16),
@@ -868,8 +875,8 @@
         pltpu.SemaphoreType.DMA((SIDE, SIDE)),
         pltpu.SemaphoreType.DMA((half // 2,)),
         pltpu.SemaphoreType.DMA((half // 2,)),
-        pltpu.SemaphoreType.DMA((8,)),
-        pltpu.SemaphoreType.DMA((8,)),
+        pltpu.SemaphoreType.DMA((9,)),
+        pltpu.SemaphoreType.DMA((9,)),
         pltpu.SemaphoreType.REGULAR((3,)),
     ]
     dispatched, slot_scale, slot_gate = pl.pallas_call(

time: 81.2 us -> 79.5 us (0.979)
  Pallas kernels: 80.4 us -> 78.7 us
    pallas_call x1, Pallas kernels: 78.9 us -> 77.3 us  [per_device(): pl.pallas_call(kernel, out_shape=(jax.ShapeDtypeStruct((experts, CAP, col...]
where the time goes in v6:
time: 79.5 us; the launch traced here: 79.4 us
  Pallas kernels  78.7 us (99%)
    pallas_call x1, Pallas kernels, per_device(): pl.pallas_call(kernel, out_shape=(jax.ShapeDtypeStruct((experts, CAP, col...  77.3 us

profile of v6, /device:TPU:513, one launch (start us, length us, event | category | flops | bytes accessed | tf_op | source)
XLA Modules:
  0.0 79.4 jit_solution(9531352477826206073)
XLA Ops:
  0.6 77.3 %shard_map.112 = (bf16[2,2,7168]{2,1,0:T(2,128)(2,1)}, f32[2,2]{1,0:T(2,128)}, f32[2,2]{1,0:T(2,128)}) custom-call(bf16[40,144]{1,0:T(8,128)(2,1)} %q_in.1, bf16[40,576,128]{2,1,0:T(8,128)(2,1)} %bitcast.4, s32[40]{0:T(128)} %ctx_in.1, bf16[128,128]{1,0:T(8,128)(2,1)} %vu_in.1, bf16[32,7168]{1,0:T(8,128)(2,1)} %op_in.1, bf16[40,56]{1,0:T(8,128)(2,1)} %res_in.1, ...), custom_call_target="tpu_custom_call" | custom-call | tf_op jit(solution)/shard_map/pallas_call | solution.py:882
  77.9 1.5 %shard_map.113 = (bf16[2,2,7168]{2,1,0:T(2,128)(2,1)}, f32[2,2]{1,0:T(2,128)}, f32[2,2]{1,0:T(2,128)}) custom-call(bf16[2,2,7168]{2,1,0:T(2,128)(2,1)} %get-tuple-element.6.refs_0_, f32[2,2]{1,0:T(2,128)} %get-tuple-element.7.refs_1_, f32[2,2]{1,0:T(2,128)} %get-tuple-element.8.refs_2_), custom_call_target="tpu_custom_call" | custom-call | tf_op jit(solution)/shard_map/pallas_call | solution.py:902

commit v7 on v6

--- a/solution.py
+++ b/solution.py
@@ -181,8 +181,9 @@
         pl.semaphore_signal(barrier, inc=1, device_id=second(p), device_id_type=MESH)
         pl.semaphore_signal(barrier, inc=1, device_id=across(p), device_id_type=MESH)
 
-    peers(a, greet)
-    peers(b, greet_second)
+    for d in FAR_FIRST:
+        greet(lax.rem(a + d, SIDE))
+        greet_second(lax.rem(b + d, SIDE))
 
     ext[...] = jnp.zeros(ext.shape, F32)
     q_load.wait()
@@ -486,9 +487,17 @@
         pl.when(c == 1)(rows)
 
     for i in range(PARTS):
-        on_core(lambda: weigh_columns(i), lambda: weigh_rows(i))
+        @pl.when(c == 0)
+        def _():
+            weigh_columns(i)
+            by_column(s1, i)
+
+        @pl.when(c == 1)
+        def _():
+            weigh_rows(i)
+            by_row(s1, i)
+
         peers(a, lambda p: mlsend(i, p).start())
-        on_core(lambda: by_column(s1, i), lambda: by_row(s1, i))
         peers(a, lambda p: osend(i, p).start())
 
 
@@ -718,8 +727,6 @@
         peers(a, lambda p: a1_from(j, p).wait_recv())
         r3[a, part_rows(j), :] = s3[a, part_rows(j), :]
         s4[part_rows(j), :] = total_of(r3, j)
-        if j == 0:
-            in_step(1)
         peers(b, lambda p: a2_send(j, p).start())
     peers(a, lambda p: q1(p).wait_send())
     loop(SIDE, lambda p: q1_across(p).wait_send())
@@ -741,8 +748,6 @@
         peers(b, lambda p: a2_from(j, p).wait_recv())
         r4[b, part_rows(j), :] = s4[part_rows(j), :]
         rf[a, part_rows(j), :] = total_of(r4, j)
-        if j == 0:
-            in_step(2)
         peers(a, lambda p: a3_send(j, p).start())
     for j in range(2):
         peers(a, lambda p: a1_send(j, p).wait_send())
@@ -877,7 +882,7 @@
         pltpu.SemaphoreType.DMA((half // 2,)),
         pltpu.SemaphoreType.DMA((9,)),
         pltpu.SemaphoreType.DMA((9,)),
-        pltpu.SemaphoreType.REGULAR((3,)),
+        pltpu.SemaphoreType.REGULAR((1,)),
     ]
     dispatched, slot_scale, slot_gate = pl.pallas_call(
         kernel,

time: 79.5 us -> 80.1 us (level)
  no operation moved by 1% of the time
where the time goes in v7:
time: 80.1 us; the launch traced here: 79.9 us
  Pallas kernels  79.3 us (99%)
    pallas_call x1, Pallas kernels, per_device(): pl.pallas_call(kernel, out_shape=(jax.ShapeDtypeStruct((experts, CAP, col...  77.8 us

profile of v7, /device:TPU:513, one launch (start us, length us, event | category | flops | bytes accessed | tf_op | source)
XLA Modules:
  0.0 79.9 jit_solution(7592689630482334283)
XLA Ops:
  0.6 77.8 %shard_map.112 = (bf16[2,2,7168]{2,1,0:T(2,128)(2,1)}, f32[2,2]{1,0:T(2,128)}, f32[2,2]{1,0:T(2,128)}) custom-call(bf16[40,144]{1,0:T(8,128)(2,1)} %q_in.1, bf16[40,576,128]{2,1,0:T(8,128)(2,1)} %bitcast.4, s32[40]{0:T(128)} %ctx_in.1, bf16[128,128]{1,0:T(8,128)(2,1)} %vu_in.1, bf16[32,7168]{1,0:T(8,128)(2,1)} %op_in.1, bf16[40,56]{1,0:T(8,128)(2,1)} %res_in.1, ...), custom_call_target="tpu_custom_call" | custom-call | tf_op jit(solution)/shard_map/pallas_call | solution.py:887
  78.4 1.5 %shard_map.113 = (bf16[2,2,7168]{2,1,0:T(2,128)(2,1)}, f32[2,2]{1,0:T(2,128)}, f32[2,2]{1,0:T(2,128)}) custom-call(bf16[2,2,7168]{2,1,0:T(2,128)(2,1)} %get-tuple-element.6.refs_0_, f32[2,2]{1,0:T(2,128)} %get-tuple-element.7.refs_1_, f32[2,2]{1,0:T(2,128)} %get-tuple-element.8.refs_2_), custom_call_target="tpu_custom_call" | custom-call | tf_op jit(solution)/shard_map/pallas_call | solution.py:907

commit v8 on v6

--- a/solution.py
+++ b/solution.py
@@ -718,8 +718,6 @@
         peers(a, lambda p: a1_from(j, p).wait_recv())
         r3[a, part_rows(j), :] = s3[a, part_rows(j), :]
         s4[part_rows(j), :] = total_of(r3, j)
-        if j == 0:
-            in_step(1)
         peers(b, lambda p: a2_send(j, p).start())
     peers(a, lambda p: q1(p).wait_send())
     loop(SIDE, lambda p: q1_across(p).wait_send())
@@ -741,8 +739,6 @@
         peers(b, lambda p: a2_from(j, p).wait_recv())
         r4[b, part_rows(j), :] = s4[part_rows(j), :]
         rf[a, part_rows(j), :] = total_of(r4, j)
-        if j == 0:
-            in_step(2)
         peers(a, lambda p: a3_send(j, p).start())
     for j in range(2):
         peers(a, lambda p: a1_send(j, p).wait_send())
@@ -877,7 +873,7 @@
         pltpu.SemaphoreType.DMA((half // 2,)),
         pltpu.SemaphoreType.DMA((9,)),
         pltpu.SemaphoreType.DMA((9,)),
-        pltpu.SemaphoreType.REGULAR((3,)),
+        pltpu.SemaphoreType.REGULAR((1,)),
     ]
     dispatched, slot_scale, slot_gate = pl.pallas_call(
         kernel,

time: 79.5 us -> 79.4 us (level)
  no operation moved by 1% of the time
where the time goes in v8:
time: 79.4 us; the launch traced here: 79.3 us
  Pallas kernels  78.6 us (99%)
    pallas_call x1, Pallas kernels, per_device(): pl.pallas_call(kernel, out_shape=(jax.ShapeDtypeStruct((experts, CAP, col...  77.2 us

profile of v8, /device:TPU:513, one launch (start us, length us, event | category | flops | bytes accessed | tf_op | source)
XLA Modules:
  0.0 79.3 jit_solution(17713171494712242862)
XLA Ops:
  0.6 77.2 %shard_map.112 = (bf16[2,2,7168]{2,1,0:T(2,128)(2,1)}, f32[2,2]{1,0:T(2,128)}, f32[2,2]{1,0:T(2,128)}) custom-call(bf16[40,144]{1,0:T(8,128)(2,1)} %q_in.1, bf16[40,576,128]{2,1,0:T(8,128)(2,1)} %bitcast.4, s32[40]{0:T(128)} %ctx_in.1, bf16[128,128]{1,0:T(8,128)(2,1)} %vu_in.1, bf16[32,7168]{1,0:T(8,128)(2,1)} %op_in.1, bf16[40,56]{1,0:T(8,128)(2,1)} %res_in.1, ...), custom_call_target="tpu_custom_call" | custom-call | tf_op jit(solution)/shard_map/pallas_call | solution.py:878
  77.8 1.5 %shard_map.113 = (bf16[2,2,7168]{2,1,0:T(2,128)(2,1)}, f32[2,2]{1,0:T(2,128)}, f32[2,2]{1,0:T(2,128)}) custom-call(bf16[2,2,7168]{2,1,0:T(2,128)(2,1)} %get-tuple-element.6.refs_0_, f32[2,2]{1,0:T(2,128)} %get-tuple-element.7.refs_1_, f32[2,2]{1,0:T(2,128)} %get-tuple-element.8.refs_2_), custom_call_target="tpu_custom_call" | custom-call | tf_op jit(solution)/shard_map/pallas_call | solution.py:898
